TPU v7x, 256 devices: a whole 4x4x8 slice. The times are simulated.
256 devices in a mesh: seq: 64 (over x, z, core), head: 4 (over y).
Axes of the slice: x: 4, y: 4, z: 8, core: 2. Of those that a mesh axis runs over, the one named last changes fastest.
Arguments:
- queries: bfloat16 [32768, 1024], P('seq', 'head'), may hold values from -6 to 6
- key_vectors: bfloat16 [32768, 1024], P('seq', 'head'), may hold values from -6 to 6
- values: bfloat16 [32768, 2048], P('seq', 'head'), may hold values from -6 to 6
- log_gate: bfloat16 [32768, 1024], P('seq', 'head'), may hold values from -1.6 to 0, as said below
- out_gate: bfloat16 [32768, 2048], P('seq', 'head'), may hold values from -6 to 6
- norm_gain: float32 [2048], P('head'), may hold values from 0.5 to 1.5
- out_weight: bfloat16 [2048, 2048], P('head'), may hold values from -0.1875 to 0.1875
Outputs:
- mixed: bfloat16 [32768, 2048], P('seq', 'head')
Inputs may be any that keep to these rules, and one draw needn't show every extreme that they name: `log_gate`: every entry is below zero.
All inputs are finite; a program needn't handle non-finite values.
Results may differ from a plain program's by a relative error of at most 0.017.
Values may be sent and summed in bfloat16 or wider, within the bound.
A program may use at most 128 MiB of HBM per device.

v0:
```python
import functools

import jax
import jax.numpy as jnp
from jax import lax
from jax.experimental import pallas as pl
from jax.experimental.pallas import tpu as pltpu
from jax.sharding import PartitionSpec as P

DK = 256
DV = 512
SPAN = 64
CHUNKS = 8
TOKENS = 64
DETOUR = 1
HOLD = 6
F32 = jnp.float32
BF16 = jnp.bfloat16
MESH = pl.DeviceIdType.MESH


def dot(a, b, dims=((1,), (0,))):
    return lax.dot_general(a, b, (dims, ((), ())), preferred_element_type=F32)


def kernel(
    n_seq, n_head,
    q_hbm, k_hbm, v_hbm, g_hbm, o_hbm, gain_hbm, w_hbm,
    out,
    q, k, v, g, o, gain, w,
    run, ends, kd, qg, att, act, state,
    log_out, log_in, half_out, half_in, own_half, chain_out, chain_in, pass_out, carry,
    gated, mine, y_out, y_in, decay, near, far,
    load_sem, w_sem, w_send, w_recv, log_sem, half_send, half_recv,
    chain_send, chain_recv, pass_send, pass_recv, g_send, g_recv, y_send, y_recv,
    near_send, near_recv, far_send, far_recv, home_send, home_recv,
):
    length = q.shape[0]
    blocks = length // SPAN
    pieces = length // TOKENS
    groups = n_head // 2
    width = w_hbm.shape[1] // n_head
    half = DK // 2
    rows = half // CHUNKS
    seq = lax.axis_index("seq")
    head = lax.axis_index("head")
    x = lax.rem(seq, 2)
    z = lax.div(seq, 2)
    last = n_seq // 2 - 1
    core = lax.rem(head, 2)
    group = lax.div(head, 2)
    across = {"seq": seq + 1 - 2 * x, "head": head}
    onward = {"seq": lax.rem(seq + 2, n_seq), "head": head}
    back = {"seq": lax.rem(seq + n_seq - 2, n_seq), "head": head}
    leads = z < last
    follows = z > 0
    partner = {"seq": seq, "head": head + 1 - 2 * core}
    peers = [
        {"seq": seq, "head": lax.rem(head + 2 * step, n_head)} for step in range(1, groups)
    ]

    def columns(which_group, which_core):
        return pl.ds(pl.multiple_of((which_group * 2 + which_core) * width, 128), width)

    loads = [
        pltpu.make_async_copy(src, dst, load_sem.at[i])
        for i, (src, dst) in enumerate(
            ((g_hbm, g), (k_hbm, k), (v_hbm, v), (q_hbm, q), (o_hbm, o), (gain_hbm, gain))
        )
    ]
    for load in loads:
        load.start()
    w_loads = [
        pltpu.make_async_copy(
            w_hbm.at[:, columns(lax.rem(group + j, groups), core)], w.at[0, j], w_sem.at[j]
        )
        for j in range(groups)
    ]
    barrier = pltpu.get_barrier_semaphore()

    def greet(friend):
        pl.semaphore_signal(barrier, inc=1, device_id=friend, device_id_type=MESH)

    for friend in [across, partner] + peers:
        greet(friend)
    pl.when(leads)(lambda: greet(onward))
    pl.when(follows)(lambda: greet(back))
    met = 2 + len(peers) + leads.astype(jnp.int32) + follows.astype(jnp.int32)

    def remote(src, dst, send, recv, device):
        return pltpu.make_async_remote_copy(
            src_ref=src, dst_ref=dst, send_sem=send, recv_sem=recv,
            device_id=device, device_id_type=MESH,
        )

    @pl.when(z == 0)
    def _():
        chain_in[...] = jnp.zeros_like(chain_in)

    tri = (
        lax.broadcasted_iota(jnp.int32, (SPAN, SPAN), 0)
        >= lax.broadcasted_iota(jnp.int32, (SPAN, SPAN), 1)
    )
    ones = jnp.where(tri, 1.0, 0.0).astype(BF16)
    loads[0].wait()
    total = jnp.zeros((1, DK), F32)
    endings = []
    for b in range(blocks):
        r = dot(ones, g[b * SPAN : (b + 1) * SPAN, :])
        run[b] = r
        endings.append(r[SPAN - 1 : SPAN, :])
        ends[b : b + 1, :] = total
        total = total + endings[b]
    log_out[...] = jnp.broadcast_to(total, log_out.shape)
    loads[1].wait()
    tail = jnp.zeros((1, DK), F32)
    for b in reversed(range(blocks)):
        part = slice(b * SPAN, (b + 1) * SPAN)
        kd[part, :] = (k[part, :].astype(F32) * jnp.exp((endings[b] - run[b]) + tail)).astype(BF16)
        tail = tail + endings[b]

    pl.semaphore_wait(barrier, met)
    log_copy = remote(log_out, log_in, log_sem.at[0], log_sem.at[1], across)
    log_copy.start()
    loads[2].wait()

    def half_state(which):
        cols = pl.ds(pl.multiple_of(which * half, 128), half)
        return dot(kd[:, cols], v[...], ((0,), (0,)))

    theirs = half_state(1 - x).astype(BF16)
    half_copies = []
    for i in range(CHUNKS):
        half_out[i] = theirs[i * rows : (i + 1) * rows, :]
        copy = remote(half_out.at[i], half_in.at[i], half_send.at[i], half_recv.at[i], across)
        copy.start()
        half_copies.append(copy)
    own_half[...] = half_state(x).reshape(CHUNKS, rows, DV)
    for load in w_loads:
        load.start()
    w_copies = [
        remote(
            w_hbm.at[:, columns(lax.rem(group + j, groups), 1 - core)], w.at[1, j],
            w_send.at[j], w_recv.at[j], partner,
        )
        for j in range(groups)
    ]
    for copy in w_copies:
        copy.start()

    for load in loads[3:]:
        load.wait()
    state[...] = jnp.zeros_like(state)

    def column(row):
        lanes = jnp.broadcast_to(row, (128, DK)).T
        return jnp.concatenate([lanes] * (DV // 128), axis=1)

    def local(b, _):
        part = pl.ds(pl.multiple_of(b * SPAN, SPAN), SPAN)
        r = run[b]
        middle = r[SPAN // 2 : SPAN // 2 + 1, :]
        ending = r[SPAN - 1 : SPAN, :]
        before = ends[pl.ds(b, 1), :]
        qf = q[part, :].astype(F32)
        kf = k[part, :].astype(F32)
        qi = qf * jnp.exp(r)
        qg[part, :] = (qi * jnp.exp(before)).astype(BF16)
        q_intra = (qf * jnp.exp(r - middle)).astype(BF16)
        k_intra = (kf * jnp.exp(middle - r)).astype(BF16)
        k_state = (kf * jnp.exp(ending - r)).astype(BF16)
        vb = v[part, :]
        scores = dot(q_intra, k_intra, ((1,), (1,)))
        weights = jnp.where(tri, scores, 0.0).astype(BF16)
        held = state[...]
        att[part, :] = dot(weights, vb) + dot(qi.astype(BF16), held.astype(BF16))
        state[...] = held * column(jnp.exp(ending)) + dot(k_state, vb, ((0,), (0,)))
        of = o[part, :].astype(F32)
        act[part, :] = of / (1.0 + jnp.exp(-of)) * gain[...]
        return 0

    early = jnp.where(leads, blocks // 2, blocks)
    lax.fori_loop(0, early, local, 0)

    log_copy.wait()
    mine_log = log_out[0:1, :]
    their_log = log_in[0:1, :]
    first = x == 0
    for i, logs in enumerate(
        (jnp.where(first, mine_log, their_log), jnp.where(first, their_log, mine_log))
    ):
        decay[i] = jnp.broadcast_to(jnp.exp(logs), (128, DK)).T

    def decays(i, at):
        lanes = decay[i, pl.ds(pl.multiple_of(x * half + at * rows, rows), rows), :]
        return jnp.concatenate([lanes] * (DV // 128), axis=1)

    chain_copies = []
    pass_copies = []
    for i in range(CHUNKS):
        half_copies[i].wait_recv()
        chain = remote(
            chain_out.at[i], chain_in.at[i], chain_send.at[i], chain_recv.at[i], onward
        )
        chain_copies.append(chain)
        own = own_half[i]
        other = half_in[i].astype(F32)
        s0 = jnp.where(first, own, other)
        s1 = jnp.where(first, other, own)

        @pl.when(follows)
        def _():
            chain.wait_recv()

        entering = chain_in[i].astype(F32)
        between = decays(0, i) * entering + s0
        chain_out[i] = (decays(1, i) * between + s1).astype(BF16)

        @pl.when(leads)
        def _():
            chain.start()

        pass_out[i] = jnp.where(first, between, entering).astype(BF16)
        carry[x, i] = jnp.where(first, entering, between).astype(BF16)
        passing = remote(
            pass_out.at[i], carry.at[x, i], pass_send.at[i], pass_recv.at[i], across
        )
        passing.start()
        pass_copies.append(passing)
    lax.fori_loop(early, blocks, local, 0)
    for passing in pass_copies:
        passing.wait_recv()
    carried = carry[...].reshape(DK, DV)

    g_copies = []
    for i in range(pieces):
        part = slice(i * TOKENS, (i + 1) * TOKENS)
        a = att[part, :] + dot(qg[part, :], carried)
        spread = jnp.mean(a * a, axis=-1, keepdims=True)
        gated[0, part, :] = (a * lax.rsqrt(spread + 1e-05) * act[part, :]).astype(BF16)
        copy = remote(
            gated.at[0, part, :], gated.at[1, part, :], g_send.at[i], g_recv.at[i], partner
        )
        copy.start()
        g_copies.append(copy)
    for copy in w_loads:
        copy.wait()
    for copy in w_copies:
        copy.wait_recv()
    first_pair = z == 0
    direct, nears, fars, homes = {}, {}, {}, {}
    for j in range(groups - 1):
        for i in range(pieces):
            part = slice(i * TOKENS, (i + 1) * TOKENS)
            direct[i, j] = remote(
                y_out.at[j, part, :], y_in.at[j, part, :],
                y_send.at[j, i], y_recv.at[j, i], peers[j],
            )
            if i < DETOUR:
                nears[i, j] = remote(
                    y_out.at[j, part, :], near.at[j, i],
                    near_send.at[j, i], near_recv.at[j, i], back,
                )
                fars[i, j] = remote(
                    near.at[j, i], far.at[j, i], far_send.at[j, i], far_recv.at[j, i], peers[j]
                )
                homes[i, j] = remote(
                    far.at[j, i], y_in.at[j, part, :],
                    home_send.at[j, i], home_recv.at[j, i], onward,
                )
    detours = sorted(nears)
    for i in range(pieces):
        part = slice(i * TOKENS, (i + 1) * TOKENS)
        g_copies[i].wait_recv()
        if i == HOLD:

            @pl.when(leads)
            def _():
                for at in detours:
                    nears[at].wait_recv()
                    fars[at].start()

        for j in range(groups - 1):
            y_out[j, part, :] = (
                dot(gated[0, part, :], w[0, j + 1]) + dot(gated[1, part, :], w[1, j + 1])
            ).astype(BF16)
            if i < DETOUR:
                pl.when(follows)(nears[i, j].start)
                pl.when(first_pair)(direct[i, j].start)
            else:
                direct[i, j].start()
    for i in range(pieces):
        part = slice(i * TOKENS, (i + 1) * TOKENS)
        mine[part, :] = dot(gated[0, part, :], w[0, 0]) + dot(gated[1, part, :], w[1, 0])

    @pl.when(leads)
    def _():
        for at in detours:
            fars[at].wait_recv()
            homes[at].start()

    for i in list(range(DETOUR, pieces)) + list(range(DETOUR)):
        part = slice(i * TOKENS, (i + 1) * TOKENS)
        total_out = mine[part, :]
        for j in range(groups - 1):
            if i < DETOUR:
                pl.when(follows)(homes[i, j].wait_recv)
                pl.when(first_pair)(direct[i, j].wait_recv)
            else:
                direct[i, j].wait_recv()
            total_out = total_out + y_in[j, part, :].astype(F32)
        out[part, :] = total_out.astype(BF16)

    @pl.when(follows)
    def _():
        for at in detours:
            nears[at].wait_send()

    @pl.when(first_pair)
    def _():
        for at in detours:
            direct[at].wait_send()

    @pl.when(leads)
    def _():
        for at in detours:
            fars[at].wait_send()
            homes[at].wait_send()

    y_copies = [direct[at] for at in direct if at not in nears]
    for copy in half_copies + pass_copies + w_copies + g_copies + y_copies:
        copy.wait_send()

    @pl.when(leads)
    def _():
        for chain in chain_copies:
            chain.wait_send()


def shards(n_seq, n_head, queries, key_vectors, values, log_gate, out_gate, norm_gain, out_weight):
    length = queries.shape[0]
    width = out_weight.shape[1] // n_head
    groups = n_head // 2
    blocks = length // SPAN
    pieces = length // TOKENS
    half_rows = DK // 2 // CHUNKS
    VM = pltpu.VMEM
    dma = pltpu.SemaphoreType.DMA
    piece_state = (CHUNKS, half_rows, DV)
    scratch = [
        VM((length, DK), BF16), VM((length, DK), BF16), VM((length, DV), BF16),
        VM((length, DK), BF16), VM((length, DV), BF16), VM((1, DV), F32),
        VM((2, groups, DV, width), BF16),
        VM((blocks, SPAN, DK), F32), VM((blocks, DK), F32), VM((length, DK), BF16),
        VM((length, DK), BF16), VM((length, DV), F32), VM((length, DV), F32), VM((DK, DV), F32),
        VM((8, DK), F32), VM((8, DK), F32), VM(piece_state, BF16), VM(piece_state, BF16),
        VM(piece_state, F32), VM(piece_state, BF16), VM(piece_state, BF16),
        VM(piece_state, BF16), VM((2,) + piece_state, BF16),
        VM((2, length, DV), BF16), VM((length, width), F32),
        VM((groups - 1, length, width), BF16), VM((groups - 1, length, width), BF16),
        VM((2, DK, 128), F32),
        VM((groups - 1, DETOUR, TOKENS, width), BF16), VM((groups - 1, DETOUR, TOKENS, width), BF16),
        dma((6,)), dma((groups,)), dma((groups,)), dma((groups,)), dma((2,)),
        dma((CHUNKS,)), dma((CHUNKS,)), dma((CHUNKS,)), dma((CHUNKS,)),
        dma((CHUNKS,)), dma((CHUNKS,)), dma((pieces,)), dma((pieces,)),
        dma((groups - 1, pieces)), dma((groups - 1, pieces)),
    ] + [dma((groups - 1, DETOUR))] * 6 + [
    ]
    return pl.pallas_call(
        functools.partial(kernel, n_seq, n_head),
        out_shape=pltpu.VMEM((length, width), BF16),
        in_specs=[pl.BlockSpec(memory_space=pl.ANY)] * 7,
        out_specs=pl.BlockSpec(memory_space=pltpu.VMEM),
        scratch_shapes=scratch,
        compiler_params=pltpu.CompilerParams(
            collective_id=0, has_side_effects=True, vmem_limit_bytes=56 * 2**20
        ),
        name="gated_layer",
    )(queries, key_vectors, values, log_gate, out_gate, norm_gain.reshape(1, DV), out_weight)


def solution(mesh):
    in_specs = (
        P("seq", "head"),
        P("seq", "head"),
        P("seq", "head"),
        P("seq", "head"),
        P("seq", "head"),
        P("head"),
        P("head", None),
    )
    out_specs = P("seq", "head")
    body = functools.partial(shards, mesh.shape["seq"], mesh.shape["head"])
    return jax.shard_map(body, mesh=mesh, in_specs=in_specs, out_specs=out_specs, check_vma=False)
```

profile of v0, /device:TPU:230, one launch (start us, length us, event | category | flops | bytes accessed | tf_op | source)
XLA Modules:
  0.0 119.4 jit_solution(11577891138555008165)
XLA Ops:
  0.0 118.6 %gated_layer.1 = bf16[512,512]{1,0:T(8,128)(2,1)S(1)} custom-call(bf16[512,256]{1,0:T(8,128)(2,1)} %q_hbm.1, bf16[512,256]{1,0:T(8,128)(2,1)} %k_hbm.1, bf16[512,512]{1,0:T(8,128)(2,1)} %v_hbm.1, bf16[512,256]{1,0:T(8,128)(2,1)} %g_hbm.1, bf16[512,512]{1,0:T(8,128)(2,1)} %o_hbm.1, f32[1,512]{1,0:T(1,128)} %bitcast.1, bf16[512,2048]{1,0:T(8,128)(2,1)} %w_hbm.1), custom_call_target="tpu_custom_call" | custom-call | tf_op jit(solution)/shard_map/gated_layer/pallas_call | solution.py:369
  118.6 0.8 copy.9
where the time goes:
time: 120 us; the launch traced here: 119 us
  Pallas kernels  119 us (99%)
    pallas_call x1, Pallas kernels, shards(): pl.pallas_call(functools.partial(kernel, n_seq, n_head), out_shape=pltpu....  119 us

commit v1 on v0

v1 whole, which is shorter than its diff:
```python
import functools

import jax
import jax.numpy as jnp
from jax import lax
from jax.experimental import pallas as pl
from jax.experimental.pallas import tpu as pltpu
from jax.sharding import PartitionSpec as P

DK = 256
DV = 512
SPAN = 64
TOKENS = 64
ROWS = 16
LANES = 128
Z = 8
EARLY = 2
F32 = jnp.float32
BF16 = jnp.bfloat16
MESH = pl.DeviceIdType.MESH


def dot(a, b, dims=((1,), (0,))):
    return lax.dot_general(a, b, (dims, ((), ())), preferred_element_type=F32)


def kernel(
    n_seq, n_head,
    q_hbm, k_hbm, v_hbm, g_hbm, o_hbm, gain_hbm, w_hbm,
    out,
    q, k, v, g, o, gain, w, w_a, w_b,
    run, ends, kd, qg, att, act, state,
    log_out, log_in, half_out, half_in, own_half, decay,
    sum_out, sum_in, sums, spans,
    tile_out, tile_in, enter_out, enter_in, pass_out, carry,
    gated, mine, y_out, y_in,
    load_sem, w_sem, w_send, w_recv, hand_send, hand_recv,
    log_send, log_recv, half_send, half_recv, pass_send, pass_recv,
    sum_send, sum_recv, tile_send, tile_recv, enter_send, enter_recv,
    g_send, g_recv, y_send, y_recv,
):
    length = q.shape[0]
    blocks = length // SPAN
    pieces = length // TOKENS
    width = w_hbm.shape[1] // n_head
    half = DK // 2
    chips = n_seq // 2
    across = DV // LANES
    seq = lax.axis_index("seq")
    head = lax.axis_index("head")
    core = lax.rem(seq, 2)
    chip = lax.div(seq, 2)
    first = core == 0
    at_x = lax.div(chip, Z)
    at_z = lax.rem(chip, Z)
    head_a = head + 1 - 2 * lax.rem(head, 2)
    head_b = n_head - 1 - head
    head_c = n_head - 1 - head_a
    sibling = {"seq": seq + 1 - 2 * core, "head": head}
    near_a = {"seq": seq, "head": head_a}
    near_b = {"seq": seq, "head": head_b}
    steps = [
        (dx, (Z // 2 + (-dz // 2 if dz % 2 else dz // 2)) % Z)
        for dz in range(Z) for dx in (2, 1, 3, 0)
    ]
    others = [
        lax.rem(at_x + dx, chips // Z) * Z + lax.rem(at_z + dz, Z)
        for dx, dz in steps if dx or dz
    ]

    def mate(other):
        return {"seq": other * 2 + core, "head": head}

    def columns(which):
        return pl.ds(pl.multiple_of(which * width, 128), width)

    loads = [
        pltpu.make_async_copy(src, dst, load_sem.at[i])
        for i, (src, dst) in enumerate(
            ((g_hbm, g), (k_hbm, k), (v_hbm, v), (q_hbm, q), (o_hbm, o), (gain_hbm, gain))
        )
    ]
    for load in loads:
        load.start()
    w_loads = [
        pltpu.make_async_copy(w_hbm.at[:, columns(which)], w.at[j], w_sem.at[j])
        for j, which in enumerate((head, head_a, head_b))
    ]
    barrier = pltpu.get_barrier_semaphore()
    friends = [mate(other) for other in others] + [sibling, near_a, near_b]
    for friend in friends:
        pl.semaphore_signal(barrier, inc=1, device_id=friend, device_id_type=MESH)

    def remote(src, dst, send, recv, device):
        return pltpu.make_async_remote_copy(
            src_ref=src, dst_ref=dst, send_sem=send, recv_sem=recv,
            device_id=device, device_id_type=MESH,
        )

    tri = (
        lax.broadcasted_iota(jnp.int32, (SPAN, SPAN), 0)
        >= lax.broadcasted_iota(jnp.int32, (SPAN, SPAN), 1)
    )
    ones = jnp.where(tri, 1.0, 0.0).astype(BF16)
    loads[0].wait()
    total = jnp.zeros((1, DK), F32)
    endings = []
    for b in range(blocks):
        r = dot(ones, g[b * SPAN : (b + 1) * SPAN, :])
        run[b] = r
        endings.append(r[SPAN - 1 : SPAN, :])
        ends[b : b + 1, :] = total
        total = total + endings[b]
    log_out[...] = jnp.broadcast_to(total, log_out.shape)
    loads[1].wait()
    tail = jnp.zeros((1, DK), F32)
    for b in reversed(range(blocks)):
        part = slice(b * SPAN, (b + 1) * SPAN)
        kd[part, :] = (k[part, :].astype(F32) * jnp.exp((endings[b] - run[b]) + tail)).astype(BF16)
        tail = tail + endings[b]
    loads[2].wait()

    def half_state(which):
        cols = pl.ds(pl.multiple_of(which * half, 128), half)
        return dot(kd[:, cols], v[...], ((0,), (0,)))

    half_out[...] = half_state(1 - core).astype(BF16)
    own_half[...] = half_state(core)

    pl.semaphore_wait(barrier, len(friends))
    log_copy = remote(log_out, log_in, log_send.at[0], log_recv.at[0], sibling)
    log_copy.start()
    half_copy = remote(half_out, half_in, half_send.at[0], half_recv.at[0], sibling)
    half_copy.start()
    w_copies = [
        remote(
            w_hbm.at[:, columns(jnp.where(first, own, head_c))], dst.at[core],
            w_send.at[j], w_recv.at[j], device,
        )
        for j, (own, dst, device) in enumerate(((head_a, w_a, near_a), (head_b, w_b, near_b)))
    ]
    hand_copies = [
        remote(dst.at[core], dst.at[core], hand_send.at[j], hand_recv.at[j], sibling)
        for j, dst in enumerate((w_a, w_b))
    ]
    for load in loads[3:]:
        load.wait()
    state[...] = jnp.zeros_like(state)

    def column(row):
        lanes = jnp.broadcast_to(row, (128, DK)).T
        return jnp.concatenate([lanes] * across, axis=1)

    def local(b, _):
        part = pl.ds(pl.multiple_of(b * SPAN, SPAN), SPAN)
        r = run[b]
        middle = r[SPAN // 2 : SPAN // 2 + 1, :]
        ending = r[SPAN - 1 : SPAN, :]
        before = ends[pl.ds(b, 1), :]
        qf = q[part, :].astype(F32)
        kf = k[part, :].astype(F32)
        qi = qf * jnp.exp(r)
        qg[part, :] = (qi * jnp.exp(before)).astype(BF16)
        q_intra = (qf * jnp.exp(r - middle)).astype(BF16)
        k_intra = (kf * jnp.exp(middle - r)).astype(BF16)
        k_state = (kf * jnp.exp(ending - r)).astype(BF16)
        vb = v[part, :]
        scores = dot(q_intra, k_intra, ((1,), (1,)))
        weights = jnp.where(tri, scores, 0.0).astype(BF16)
        held = state[...]
        att[part, :] = dot(weights, vb) + dot(qi.astype(BF16), held.astype(BF16))
        state[...] = held * column(jnp.exp(ending)) + dot(k_state, vb, ((0,), (0,)))
        of = o[part, :].astype(F32)
        act[part, :] = of / (1.0 + jnp.exp(-of)) * gain[...]
        return 0

    log_copy.wait_recv()
    both = [jnp.where(first, row[:, :half], row[:, half:]) for row in (log_out[0:1, :], log_in[0:1, :])]
    sum_out[...] = both[0] + both[1]
    sum_copies = [
        remote(sum_out, sum_in.at[chip], sum_send.at[i], sum_recv.at[i], mate(other))
        for i, other in enumerate(others)
    ]
    for copy in sum_copies:
        copy.start()
    sum_in[chip] = sum_out[...]
    for i, row in enumerate(
        (jnp.where(first, both[0], both[1]), jnp.where(first, both[1], both[0]))
    ):
        decay[i] = jnp.broadcast_to(jnp.exp(row), (128, half)).T

    def decays(i, rows):
        return jnp.concatenate([decay[i, rows, :]] * across, axis=1)

    def halves(rows):
        own = own_half[rows, :]
        other = half_in[rows, :].astype(F32)
        return jnp.where(first, own, other), jnp.where(first, other, own)

    half_copy.wait_recv()
    for i in range(half // ROWS):
        rows = slice(i * ROWS, (i + 1) * ROWS)
        s0, s1 = halves(rows)
        chip_state = (decays(1, rows) * s0 + s1).astype(BF16)
        for j in range(across):
            tile_out[i * across + j] = chip_state[:, j * LANES : (j + 1) * LANES]
    tile_copies = [
        remote(tile_out.at[other], tile_in.at[chip], tile_send.at[i], tile_recv.at[i], mate(other))
        for i, other in enumerate(others)
    ]
    for copy in tile_copies:
        copy.start()
    tile_in[chip] = tile_out[chip]
    for copy in w_copies + w_loads:
        copy.start()

    lax.fori_loop(0, blocks, local, 0)

    for copy in sum_copies:
        copy.wait_recv()
    sums[...] = jnp.zeros_like(sums)
    for i in range(chips):
        sums[i : i + 1, :] = sum_in[i]
    spans[...] = jnp.exp(sums[...].T)
    mine_rows = pl.ds(pl.multiple_of(lax.div(chip, across) * ROWS, ROWS), ROWS)
    factors = spans[mine_rows, :]
    factor = [jnp.broadcast_to(factors[:, i : i + 1], (ROWS, LANES)) for i in range(chips)]
    for copy in tile_copies:
        copy.wait_recv()
    entering = jnp.zeros((ROWS, LANES), F32)
    for i in range(chips):
        enter_out[i] = entering.astype(BF16)
        entering = factor[i] * entering + tile_in[i].astype(F32)
    enter_copies = [
        remote(enter_out.at[other], enter_in.at[chip], enter_send.at[i], enter_recv.at[i], mate(other))
        for i, other in enumerate(others)
    ]
    for copy in enter_copies:
        copy.start()
    enter_in[chip] = enter_out[chip]

    for copy, hand in zip(w_copies, hand_copies):
        copy.wait_recv()
        hand.start()

    for copy in enter_copies:
        copy.wait_recv()
    for i in range(half // ROWS):
        rows = slice(i * ROWS, (i + 1) * ROWS)
        s0, _ = halves(rows)
        entry = jnp.concatenate(
            [enter_in[i * across + j] for j in range(across)], axis=1
        ).astype(F32)
        between = decays(0, rows) * entry + s0
        pass_out[rows, :] = jnp.where(first, between, entry).astype(BF16)
        carry[core, rows, :] = jnp.where(first, entry, between).astype(BF16)
    pass_copy = remote(pass_out, carry.at[core], pass_send.at[0], pass_recv.at[0], sibling)
    pass_copy.start()
    pass_copy.wait_recv()
    carried = carry[...].reshape(DK, DV)

    split = pieces // 2
    order = [i + j * split for i in range(split) for j in range(2)]
    parts = [slice(i * TOKENS, (i + 1) * TOKENS) for i in range(pieces)]
    g_copies = [
        remote(
            gated.at[0, parts[i], :], gated.at[1, parts[i], :], g_send.at[i], g_recv.at[i],
            near_a if i < split else near_b,
        )
        for i in range(pieces)
    ]
    y_copies = [
        remote(
            y_out.at[parts[i], :], y_in.at[parts[i], :], y_send.at[i], y_recv.at[i],
            near_b if i < split else near_a,
        )
        for i in range(pieces)
    ]
    for i in order:
        part = parts[i]
        a = att[part, :] + dot(qg[part, :], carried)
        spread = jnp.mean(a * a, axis=-1, keepdims=True)
        gated[0, part, :] = (a * lax.rsqrt(spread + 1e-05) * act[part, :]).astype(BF16)
        g_copies[i].start()
    for copy in w_loads:
        copy.wait()
    for copy in hand_copies:
        copy.wait_recv()
    for i in order:
        part = parts[i]
        g_copies[i].wait_recv()
        own_w, far_w = (w.at[2], w_a) if i < split else (w.at[1], w_b)
        y_out[part, :] = (
            dot(gated[0, part, :], own_w[...]) + dot(gated[1, part, :], far_w[1])
        ).astype(BF16)
        y_copies[i].start()
    for i in order:
        part = parts[i]
        far_w = w_a if i < split else w_b
        mine[part, :] = dot(gated[0, part, :], w[0]) + dot(gated[1, part, :], far_w[0])
    for i in order:
        part = parts[i]
        y_copies[i].wait_recv()
        out[part, :] = (mine[part, :] + y_in[part, :].astype(F32)).astype(BF16)

    for copy in (
        [log_copy, half_copy, pass_copy] + w_copies + hand_copies
        + sum_copies + tile_copies + enter_copies + g_copies + y_copies
    ):
        copy.wait_send()


def shards(n_seq, n_head, queries, key_vectors, values, log_gate, out_gate, norm_gain, out_weight):
    length = queries.shape[0]
    width = out_weight.shape[1] // n_head
    blocks = length // SPAN
    pieces = length // TOKENS
    chips = n_seq // 2
    half = DK // 2
    VM = pltpu.VMEM
    dma = pltpu.SemaphoreType.DMA
    tiles = VM((chips, ROWS, LANES), BF16)
    scratch = [
        VM((length, DK), BF16), VM((length, DK), BF16), VM((length, DV), BF16),
        VM((length, DK), BF16), VM((length, DV), BF16), VM((1, DV), F32),
        VM((3, DV, width), BF16), VM((2, DV, width), BF16), VM((2, DV, width), BF16),
        VM((blocks, SPAN, DK), F32), VM((blocks, DK), F32), VM((length, DK), BF16),
        VM((length, DK), BF16), VM((length, DV), F32), VM((length, DV), F32), VM((DK, DV), F32),
        VM((8, DK), F32), VM((8, DK), F32), VM((half, DV), BF16), VM((half, DV), BF16),
        VM((half, DV), F32), VM((2, half, 128), F32),
        VM((1, half), F32), VM((chips, 1, half), F32), VM((128, half), F32), VM((half, 128), F32),
        tiles, tiles, tiles, tiles, VM((half, DV), BF16), VM((2, half, DV), BF16),
        VM((2, length, DV), BF16), VM((length, width), F32),
        VM((length, width), BF16), VM((length, width), BF16),
        dma((6,)), dma((3,)), dma((2,)), dma((2,)), dma((2,)), dma((2,)),
        dma((1,)), dma((1,)), dma((1,)), dma((1,)), dma((1,)), dma((1,)),
        dma((chips - 1,)), dma((chips - 1,)), dma((chips - 1,)), dma((chips - 1,)),
        dma((chips - 1,)), dma((chips - 1,)),
        dma((pieces,)), dma((pieces,)), dma((pieces,)), dma((pieces,)),
    ]
    return pl.pallas_call(
        functools.partial(kernel, n_seq, n_head),
        out_shape=pltpu.VMEM((length, width), BF16),
        in_specs=[pl.BlockSpec(memory_space=pl.ANY)] * 7,
        out_specs=pl.BlockSpec(memory_space=pltpu.VMEM),
        scratch_shapes=scratch,
        compiler_params=pltpu.CompilerParams(
            collective_id=0, has_side_effects=True, vmem_limit_bytes=56 * 2**20
        ),
        name="gated_layer",
    )(queries, key_vectors, values, log_gate, out_gate, norm_gain.reshape(1, DV), out_weight)


def solution(mesh):
    in_specs = (
        P("seq", "head"),
        P("seq", "head"),
        P("seq", "head"),
        P("seq", "head"),
        P("seq", "head"),
        P("head"),
        P("head", None),
    )
    out_specs = P("seq", "head")
    body = functools.partial(shards, mesh.shape["seq"], mesh.shape["head"])
    return jax.shard_map(body, mesh=mesh, in_specs=in_specs, out_specs=out_specs, check_vma=False)
```

time: 120 us -> 46.3 us (0.39)
  the two profiles are of different devices: /device:TPU:230 before, /device:TPU:1 now
where the time goes in v1:
time: 46.3 us; the launch traced here: 46.2 us
  Pallas kernels  45.4 us (98%)
  local copies, waits for them, and re-layouts  0.8 us (2%)
    pallas_call x1, Pallas kernels, shards(): pl.pallas_call(functools.partial(kernel, n_seq, n_head), out_shape=pltpu....  45.4 us

profile of v1, /device:TPU:1, one launch (start us, length us, event | category | flops | bytes accessed | tf_op | source)
XLA Modules:
  0.0 46.2 jit_solution(2567965825220648213)
XLA Ops:
  0.0 45.4 %gated_layer.1 = bf16[512,512]{1,0:T(8,128)(2,1)S(1)} custom-call(bf16[512,256]{1,0:T(8,128)(2,1)} %q_hbm.1, bf16[512,256]{1,0:T(8,128)(2,1)} %k_hbm.1, bf16[512,512]{1,0:T(8,128)(2,1)} %v_hbm.1, bf16[512,256]{1,0:T(8,128)(2,1)} %g_hbm.1, bf16[512,512]{1,0:T(8,128)(2,1)} %o_hbm.1, f32[1,512]{1,0:T(1,128)} %bitcast.1, bf16[512,2048]{1,0:T(8,128)(2,1)} %w_hbm.1), custom_call_target="tpu_custom_call" | custom-call | tf_op jit(solution)/shard_map/gated_layer/pallas_call | solution.py:341
  45.4 0.8 %copy.9 = bf16[512,512]{1,0:T(8,128)(2,1)} copy(bf16[512,512]{1,0:T(8,128)(2,1)S(1)} %gated_layer.1) | data formatting | bytes 1048576

commit v2 on v1

v2 whole, which is shorter than its diff:
```python
import functools

import jax
import jax.numpy as jnp
from jax import lax
from jax.experimental import pallas as pl
from jax.experimental.pallas import tpu as pltpu
from jax.sharding import PartitionSpec as P

DK = 256
DV = 512
SPAN = 64
TOKENS = 64
Z = 8
F32 = jnp.float32
BF16 = jnp.bfloat16
MESH = pl.DeviceIdType.MESH


def dot(a, b, dims=((1,), (0,))):
    return lax.dot_general(a, b, (dims, ((), ())), preferred_element_type=F32)


def kernel(
    n_seq, n_head,
    q_hbm, k_hbm, v_hbm, g_hbm, o_hbm, gain_hbm, w_hbm,
    out,
    q, k, v, g, o, gain, w, w_a, w_b,
    run, ends, kd, qg, att, act, state,
    log_out, log_in, own_state, core_out, core_in, decay,
    sum_out, sum_in, row_out, row_in, sums, spans, row_spans,
    tile_out, tile_in, total_out, total_in, ahead, enter_out, enter_in, carry,
    gated, mine, y_out, y_in,
    load_sem, w_sem, w_send, w_recv, hand_send, hand_recv,
    log_send, log_recv, core_send, core_recv,
    sum_send, sum_recv, row_send, row_recv, tile_send, tile_recv,
    total_send, total_recv, enter_send, enter_recv, pass_send, pass_recv,
    g_send, g_recv, y_send, y_recv,
):
    length = q.shape[0]
    blocks = length // SPAN
    pieces = length // TOKENS
    width = w_hbm.shape[1] // n_head
    rows_x = n_seq // 2 // Z
    part_rows = DK // Z
    copies = DV // 128
    seq = lax.axis_index("seq")
    head = lax.axis_index("head")
    core = lax.rem(seq, 2)
    chip = lax.div(seq, 2)
    feeds = core == 0
    scans = core == 1
    at_x = lax.div(chip, Z)
    at_z = lax.rem(chip, Z)
    head_a = head + 1 - 2 * lax.rem(head, 2)
    head_b = n_head - 1 - head
    head_c = n_head - 1 - head_a
    sibling = {"seq": seq + 1 - 2 * core, "head": head}
    near_a = {"seq": seq, "head": head_a}
    near_b = {"seq": seq, "head": head_b}
    row_z = [lax.rem(at_z + dz, Z) for dz in sorted(range(1, Z), key=lambda d: abs(d - Z // 2))]
    from_z = [lax.rem(at_z + Z - dz, Z) for dz in sorted(range(1, Z), key=lambda d: abs(d - Z // 2))]

    def mate(x, z):
        return {"seq": (x * Z + z) * 2 + core, "head": head}

    in_row = [mate(at_x, z) for z in row_z]
    later = [mate(lax.rem(at_x + dx, rows_x), at_z) for dx in range(1, rows_x)]

    def columns(which):
        return pl.ds(pl.multiple_of(which * width, 128), width)

    def remote(src, dst, send, recv, device):
        return pltpu.make_async_remote_copy(
            src_ref=src, dst_ref=dst, send_sem=send, recv_sem=recv,
            device_id=device, device_id_type=MESH,
        )

    barrier = pltpu.get_barrier_semaphore()

    def greet(friends):
        for friend in friends:
            pl.semaphore_signal(barrier, inc=1, device_id=friend, device_id_type=MESH)

    near = [sibling, near_a, near_b]
    greet(near)
    pl.when(scans)(lambda: greet(in_row + later))
    loads = [
        pltpu.make_async_copy(src, dst, load_sem.at[i])
        for i, (src, dst) in enumerate(
            ((g_hbm, g), (k_hbm, k), (v_hbm, v), (q_hbm, q), (o_hbm, o), (gain_hbm, gain))
        )
    ]
    for load in loads:
        load.start()
    w_loads = [
        pltpu.make_async_copy(w_hbm.at[:, columns(which)], w.at[j], w_sem.at[j])
        for j, which in enumerate((head, head_a, head_b))
    ]
    w_copies = [
        remote(w_hbm.at[:, columns(which)], dst.at[j], w_send.at[i], w_recv.at[i], device)
        for i, (which, dst, j, device) in enumerate((
            (head_c, w_a, 1, near_a), (head_c, w_b, 1, near_b),
            (head_a, w_a, 0, near_a), (head_b, w_b, 0, near_b),
        ))
    ]
    hand_copies = [
        remote(dst.at[j], dst.at[j], hand_send.at[i], hand_recv.at[i], sibling)
        for i, (dst, j) in enumerate(((w_a, 1), (w_b, 1), (w_a, 0), (w_b, 0)))
    ]
    log_copy = remote(log_out, log_in, log_send.at[0], log_recv.at[0], sibling)
    core_copy = remote(core_out, core_in, core_send.at[0], core_recv.at[0], sibling)

    @pl.when(feeds)
    def _():
        pl.semaphore_wait(barrier, len(near))
        for copy in w_copies:
            copy.start()

    tri = (
        lax.broadcasted_iota(jnp.int32, (SPAN, SPAN), 0)
        >= lax.broadcasted_iota(jnp.int32, (SPAN, SPAN), 1)
    )
    ones = jnp.where(tri, 1.0, 0.0).astype(BF16)
    loads[0].wait()
    total = jnp.zeros((1, DK), F32)
    endings = []
    for b in range(blocks):
        r = dot(ones, g[b * SPAN : (b + 1) * SPAN, :])
        run[b] = r
        endings.append(r[SPAN - 1 : SPAN, :])
        ends[b : b + 1, :] = total
        total = total + endings[b]
    log_out[...] = total
    pl.when(feeds)(log_copy.start)
    loads[1].wait()
    tail = jnp.zeros((1, DK), F32)
    for b in reversed(range(blocks)):
        part = slice(b * SPAN, (b + 1) * SPAN)
        kd[part, :] = (k[part, :].astype(F32) * jnp.exp((endings[b] - run[b]) + tail)).astype(BF16)
        tail = tail + endings[b]
    loads[2].wait()
    for cols in (slice(0, DK // 2), slice(DK // 2, DK)):
        grown = dot(kd[:, cols], v[...], ((0,), (0,)))
        own_state[cols, :] = grown
        core_out[cols, :] = grown.astype(BF16)
    pl.when(feeds)(core_copy.start)
    for load in w_loads:
        load.start()

    def lanes(row):
        return jnp.broadcast_to(row, (128, DK)).T

    def wide(columns):
        return jnp.concatenate([columns] * copies, axis=1)

    def part_of(z):
        return slice(z * part_rows, (z + 1) * part_rows)

    sum_copies = [
        remote(sum_out, sum_in.at[at_z], sum_send.at[i], sum_recv.at[i], device)
        for i, device in enumerate(in_row)
    ]
    tile_copies = [
        remote(tile_out.at[z], tile_in.at[at_z], tile_send.at[i], tile_recv.at[i], device)
        for i, (z, device) in enumerate(zip(row_z, in_row))
    ]
    row_copies = [
        remote(row_out, row_in.at[at_x], row_send.at[i], row_recv.at[i], device)
        for i, device in enumerate(later)
    ]
    total_copies = [
        remote(total_out, total_in.at[at_x], total_send.at[i], total_recv.at[i], device)
        for i, device in enumerate(later)
    ]
    enter_copies = [
        remote(enter_out.at[z], enter_in.at[at_z], enter_send.at[i], enter_recv.at[i], device)
        for i, (z, device) in enumerate(zip(row_z, in_row))
    ]
    pass_copies = [
        remote(enter_in.at[z], carry.at[z], pass_send.at[i], pass_recv.at[i], sibling)
        for i, z in enumerate([at_z] + from_z)
    ]

    @pl.when(scans)
    def _():
        log_copy.wait_recv()
        sum_out[...] = log_out[...] + log_in[...]
        decay[0] = lanes(jnp.exp(log_in[...]))
        decay[1] = lanes(jnp.exp(log_out[...]))
        core_copy.wait_recv()
        for z in range(Z):
            part = part_of(z)
            tile_out[z] = (
                wide(decay[1, part, :]) * core_in[part, :].astype(F32) + own_state[part, :]
            ).astype(BF16)
        sum_in[at_z] = sum_out[...]
        tile_in[at_z] = tile_out[at_z]
        pl.semaphore_wait(barrier, len(near) + len(in_row) + len(later))
        for copy in sum_copies + tile_copies:
            copy.start()

    for load in loads[3:]:
        load.wait()
    state[...] = jnp.zeros_like(state)

    def local(b, _):
        part = pl.ds(pl.multiple_of(b * SPAN, SPAN), SPAN)
        r = run[b]
        middle = r[SPAN // 2 : SPAN // 2 + 1, :]
        ending = r[SPAN - 1 : SPAN, :]
        before = ends[pl.ds(b, 1), :]
        qf = q[part, :].astype(F32)
        kf = k[part, :].astype(F32)
        qi = qf * jnp.exp(r)
        qg[part, :] = (qi * jnp.exp(before)).astype(BF16)
        q_intra = (qf * jnp.exp(r - middle)).astype(BF16)
        k_intra = (kf * jnp.exp(middle - r)).astype(BF16)
        k_state = (kf * jnp.exp(ending - r)).astype(BF16)
        vb = v[part, :]
        scores = dot(q_intra, k_intra, ((1,), (1,)))
        weights = jnp.where(tri, scores, 0.0).astype(BF16)
        held = state[...]
        att[part, :] = dot(weights, vb) + dot(qi.astype(BF16), held.astype(BF16))
        state[...] = held * wide(lanes(jnp.exp(ending))) + dot(k_state, vb, ((0,), (0,)))
        of = o[part, :].astype(F32)
        act[part, :] = of / (1.0 + jnp.exp(-of)) * gain[...]
        return 0

    lax.fori_loop(0, blocks, local, 0)

    @pl.when(scans)
    def _():
        sums[...] = jnp.zeros_like(sums)
        for copy in sum_copies:
            copy.wait_recv()
        along = jnp.zeros((1, DK), F32)
        for z in range(Z):
            sums[z : z + 1, :] = sum_in[z]
            along = along + sum_in[z]
        row_out[...] = along
        for i, copy in enumerate(row_copies):
            pl.when(at_x + i + 1 < rows_x)(copy.start)
        spans[...] = jnp.exp(sums[...].T)
        own_rows = pl.ds(pl.multiple_of(at_z * part_rows, part_rows), part_rows)

        def factor(table, i):
            return wide(jnp.broadcast_to(table[own_rows, :][:, i : i + 1], (part_rows, 128)))

        for copy in tile_copies:
            copy.wait_recv()
        grown = tile_in[0].astype(F32)
        for z in range(1, Z):
            grown = factor(spans, z) * grown + tile_in[z].astype(F32)
        total_out[...] = grown.astype(BF16)
        for i, copy in enumerate(total_copies):
            pl.when(at_x + i + 1 < rows_x)(copy.start)
        ahead[...] = jnp.zeros_like(ahead)
        for x in range(rows_x - 1):

            @pl.when(at_x > x)
            def _():
                for i in range(rows_x - 1):
                    pl.when(at_x == x + i + 1)(row_copies[i].wait_recv)
                sums[Z + x : Z + x + 1, :] = row_in[x]

        @pl.when(at_x > 0)
        def _():
            row_spans[...] = jnp.exp(sums[...].T)

        for x in range(rows_x - 1):

            @pl.when(at_x > x)
            def _():
                for i in range(rows_x - 1):
                    pl.when(at_x == x + i + 1)(total_copies[i].wait_recv)
                ahead[...] = factor(row_spans, Z + x) * ahead[...] + total_in[x].astype(F32)

        entry = ahead[...]
        for z in range(Z):
            enter_out[z] = entry.astype(BF16)
            if z < Z - 1:
                entry = factor(spans, z) * entry + tile_in[z].astype(F32)
        for copy in enter_copies:
            copy.start()
        enter_in[at_z] = enter_out[at_z]
        pass_copies[0].start()
        for copy, onward in zip(enter_copies, pass_copies[1:]):
            copy.wait_recv()
            onward.start()
        for z in range(Z):
            part = part_of(z)
            carry[z] = (
                wide(decay[0, part, :]) * enter_in[z].astype(F32) + core_in[part, :].astype(F32)
            ).astype(BF16)

    @pl.when(feeds)
    def _():
        for copy, hand in zip(w_copies, hand_copies):
            copy.wait_recv()
            hand.start()
        for copy in pass_copies:
            copy.wait_recv()

    carried = carry[...].reshape(DK, DV)

    split = pieces // 2
    order = [i + j * split for i in range(split) for j in range(2)]
    parts = [slice(i * TOKENS, (i + 1) * TOKENS) for i in range(pieces)]
    g_copies = [
        remote(
            gated.at[0, parts[i], :], gated.at[1, parts[i], :], g_send.at[i], g_recv.at[i],
            near_a if i < split else near_b,
        )
        for i in range(pieces)
    ]
    y_copies = [
        remote(
            y_out.at[parts[i], :], y_in.at[parts[i], :], y_send.at[i], y_recv.at[i],
            near_b if i < split else near_a,
        )
        for i in range(pieces)
    ]
    for i in order:
        part = parts[i]
        a = att[part, :] + dot(qg[part, :], carried)
        spread = jnp.mean(a * a, axis=-1, keepdims=True)
        gated[0, part, :] = (a * lax.rsqrt(spread + 1e-05) * act[part, :]).astype(BF16)
        g_copies[i].start()
    for copy in w_loads:
        copy.wait()

    @pl.when(scans)
    def _():
        for copy in hand_copies:
            copy.wait_recv()

    for i in order:
        part = parts[i]
        g_copies[i].wait_recv()
        own_w, far_w = (w.at[2], w_a) if i < split else (w.at[1], w_b)
        y_out[part, :] = (
            dot(gated[0, part, :], own_w[...]) + dot(gated[1, part, :], far_w[1])
        ).astype(BF16)
        y_copies[i].start()
    for i in order:
        part = parts[i]
        far_w = w_a if i < split else w_b
        mine[part, :] = dot(gated[0, part, :], w[0]) + dot(gated[1, part, :], far_w[0])
    for i in order:
        part = parts[i]
        y_copies[i].wait_recv()
        out[part, :] = (mine[part, :] + y_in[part, :].astype(F32)).astype(BF16)

    for copy in g_copies + y_copies:
        copy.wait_send()

    @pl.when(feeds)
    def _():
        for copy in [log_copy, core_copy] + w_copies + hand_copies:
            copy.wait_send()

    @pl.when(scans)
    def _():
        for copy in sum_copies + tile_copies + enter_copies + pass_copies:
            copy.wait_send()
        for i in range(rows_x - 1):

            @pl.when(at_x + i + 1 < rows_x)
            def _():
                row_copies[i].wait_send()
                total_copies[i].wait_send()


def shards(n_seq, n_head, queries, key_vectors, values, log_gate, out_gate, norm_gain, out_weight):
    length = queries.shape[0]
    width = out_weight.shape[1] // n_head
    blocks = length // SPAN
    pieces = length // TOKENS
    rows_x = n_seq // 2 // Z
    VM = pltpu.VMEM
    dma = pltpu.SemaphoreType.DMA
    tiles = VM((Z, DK // Z, DV), BF16)
    row = VM((1, DK), F32)
    scratch = [
        VM((length, DK), BF16), VM((length, DK), BF16), VM((length, DV), BF16),
        VM((length, DK), BF16), VM((length, DV), BF16), VM((1, DV), F32),
        VM((3, DV, width), BF16), VM((2, DV, width), BF16), VM((2, DV, width), BF16),
        VM((blocks, SPAN, DK), F32), VM((blocks, DK), F32), VM((length, DK), BF16),
        VM((length, DK), BF16), VM((length, DV), F32), VM((length, DV), F32), VM((DK, DV), F32),
        row, row, VM((DK, DV), F32), VM((DK, DV), BF16), VM((DK, DV), BF16), VM((2, DK, 128), F32),
        row, VM((Z, 1, DK), F32), row, VM((rows_x, 1, DK), F32),
        VM((128, DK), F32), VM((DK, 128), F32), VM((DK, 128), F32),
        tiles, tiles, VM((DK // Z, DV), BF16), VM((rows_x, DK // Z, DV), BF16),
        VM((DK // Z, DV), F32), tiles, tiles, tiles,
        VM((2, length, DV), BF16), VM((length, width), F32),
        VM((length, width), BF16), VM((length, width), BF16),
        dma((6,)), dma((3,)), dma((4,)), dma((4,)), dma((4,)), dma((4,)),
        dma((1,)), dma((1,)), dma((1,)), dma((1,)),
        dma((Z - 1,)), dma((Z - 1,)), dma((rows_x - 1,)), dma((rows_x - 1,)),
        dma((Z - 1,)), dma((Z - 1,)), dma((rows_x - 1,)), dma((rows_x - 1,)),
        dma((Z - 1,)), dma((Z - 1,)), dma((Z,)), dma((Z,)),
        dma((pieces,)), dma((pieces,)), dma((pieces,)), dma((pieces,)),
    ]
    return pl.pallas_call(
        functools.partial(kernel, n_seq, n_head),
        out_shape=pltpu.VMEM((length, width), BF16),
        in_specs=[pl.BlockSpec(memory_space=pl.ANY)] * 7,
        out_specs=pl.BlockSpec(memory_space=pltpu.VMEM),
        scratch_shapes=scratch,
        compiler_params=pltpu.CompilerParams(
            collective_id=0, has_side_effects=True, vmem_limit_bytes=56 * 2**20
        ),
        name="gated_layer",
    )(queries, key_vectors, values, log_gate, out_gate, norm_gain.reshape(1, DV), out_weight)


def solution(mesh):
    in_specs = (
        P("seq", "head"),
        P("seq", "head"),
        P("seq", "head"),
        P("seq", "head"),
        P("seq", "head"),
        P("head"),
        P("head", None),
    )
    out_specs = P("seq", "head")
    body = functools.partial(shards, mesh.shape["seq"], mesh.shape["head"])
    return jax.shard_map(body, mesh=mesh, in_specs=in_specs, out_specs=out_specs, check_vma=False)
```

time: 46.3 us -> 38.2 us (0.83)
  the two profiles are of different devices: /device:TPU:1 before, /device:TPU:6 now
where the time goes in v2:
time: 38.2 us; the launch traced here: 38.1 us
  Pallas kernels  37.3 us (98%)
  local copies, waits for them, and re-layouts  0.8 us (2%)
    pallas_call x1, Pallas kernels, shards(): pl.pallas_call(functools.partial(kernel, n_seq, n_head), out_shape=pltpu....  37.3 us
    unnamed x1, local copies, waits for them, and re-layouts  0.8 us

profile of v2, /device:TPU:6, one launch (start us, length us, event | category | flops | bytes accessed | tf_op | source)
XLA Modules:
  0.0 38.1 jit_solution(15954806808332353873)
XLA Ops:
  0.0 37.3 %gated_layer.1 = bf16[512,512]{1,0:T(8,128)(2,1)S(1)} custom-call(bf16[512,256]{1,0:T(8,128)(2,1)} %q_hbm.1, bf16[512,256]{1,0:T(8,128)(2,1)} %k_hbm.1, bf16[512,512]{1,0:T(8,128)(2,1)} %v_hbm.1, bf16[512,256]{1,0:T(8,128)(2,1)} %g_hbm.1, bf16[512,512]{1,0:T(8,128)(2,1)} %o_hbm.1, f32[1,512]{1,0:T(1,128)} %bitcast.1, bf16[512,2048]{1,0:T(8,128)(2,1)} %w_hbm.1), custom_call_target="tpu_custom_call" | custom-call | tf_op jit(solution)/shard_map/gated_layer/pallas_call | solution.py:405
  37.4 0.8 %copy.9 = bf16[512,512]{1,0:T(8,128)(2,1)} copy(bf16[512,512]{1,0:T(8,128)(2,1)S(1)} %gated_layer.1) | data formatting | bytes 1048576

commit v3 on v2

v3 whole, which is shorter than its diff:
```python
import functools

import jax
import jax.numpy as jnp
from jax import lax
from jax.experimental import pallas as pl
from jax.experimental.pallas import tpu as pltpu
from jax.sharding import PartitionSpec as P

DK = 256
DV = 512
SPAN = 64
TOKENS = 64
Z = 8
F32 = jnp.float32
BF16 = jnp.bfloat16
MESH = pl.DeviceIdType.MESH


def dot(a, b, dims=((1,), (0,))):
    return lax.dot_general(a, b, (dims, ((), ())), preferred_element_type=F32)


def kernel(
    n_seq, n_head,
    q_hbm, k_hbm, v_hbm, g_hbm, o_hbm, gain_hbm, w_hbm,
    out,
    q, k, v, g, o, gain, w, w_near,
    run, ends, kd, qg, att, act, state,
    log_out, log_in, own_state, core_out, core_in, decay,
    sum_out, sum_in, row_out, row_in, sums, spans, row_spans,
    tile_out, tile_in, total_out, total_in, ahead, enter_out, enter_in, carry,
    gated, mine, y_out, y_in,
    load_sem, w_sem, w_send, w_recv, hand_send, hand_recv,
    log_send, log_recv, core_send, core_recv,
    sum_send, sum_recv, row_send, row_recv, tile_send, tile_recv,
    total_send, total_recv, enter_send, enter_recv, pass_send, pass_recv,
    g_send, g_recv, y_send, y_recv,
):
    loads = [
        pltpu.make_async_copy(src, dst, load_sem.at[i])
        for i, (src, dst) in enumerate(
            ((g_hbm, g), (k_hbm, k), (v_hbm, v), (q_hbm, q), (o_hbm, o), (gain_hbm, gain))
        )
    ]
    for load in loads[:3]:
        load.start()
    length = q.shape[0]
    blocks = length // SPAN
    pieces = length // TOKENS
    width = w_hbm.shape[1] // n_head
    rows_x = n_seq // 2 // Z
    part_rows = DK // Z
    copies = DV // 128
    seq = lax.axis_index("seq")
    head = lax.axis_index("head")
    core = lax.rem(seq, 2)
    chip = lax.div(seq, 2)
    feeds = core == 0
    scans = core == 1
    at_x = lax.div(chip, Z)
    at_z = lax.rem(chip, Z)
    head_a = head + 1 - 2 * lax.rem(head, 2)
    head_b = n_head - 1 - head
    head_c = n_head - 1 - head_a
    sibling = {"seq": seq + 1 - 2 * core, "head": head}
    near_a = {"seq": seq, "head": head_a}
    near_b = {"seq": seq, "head": head_b}

    def mate(x, z):
        return {"seq": (x * Z + z) * 2 + core, "head": head}

    in_row = [mate(at_x, lax.rem(at_z + dz, Z)) for dz in range(1, Z)]
    later = {dx: mate(lax.rem(at_x + dx, rows_x), at_z) for dx in (2, 1, 3)}

    def columns(which):
        return pl.ds(pl.multiple_of(which * width, 128), width)

    def remote(src, dst, send, recv, device):
        return pltpu.make_async_remote_copy(
            src_ref=src, dst_ref=dst, send_sem=send, recv_sem=recv,
            device_id=device, device_id_type=MESH,
        )

    def landed(ref, sem):
        pltpu.make_async_copy(ref, ref, sem).wait()

    barrier = pltpu.get_barrier_semaphore()

    def greet(friends):
        for friend in friends:
            pl.semaphore_signal(barrier, inc=1, device_id=friend, device_id_type=MESH)

    near = [sibling, near_a, near_b]
    greet(near)
    pl.when(scans)(lambda: greet(in_row + list(later.values())))
    w_loads = [
        pltpu.make_async_copy(w_hbm.at[:, columns(which)], w.at[j], w_sem.at[0])
        for j, which in enumerate((head, head_a, head_b))
    ]
    w_copies = [
        remote(w_hbm.at[:, columns(which)], w_near.at[j, i], w_send.at[0], w_recv.at[j], device)
        for which, j, i, device in (
            (head_c, 1, 0, near_a), (head_c, 1, 1, near_b),
            (head_a, 0, 0, near_a), (head_b, 0, 1, near_b),
        )
    ]
    hand_copies = [
        remote(w_near.at[j], w_near.at[j], hand_send.at[0], hand_recv.at[0], sibling) for j in (1, 0)
    ]
    log_copy = remote(log_out, log_in, log_send.at[0], log_recv.at[0], sibling)
    channels = [slice(0, DK // 2), slice(DK // 2, DK)]
    core_copies = [
        remote(core_out.at[cols, :], core_in.at[cols, :], core_send.at[0], core_recv.at[i], sibling)
        for i, cols in enumerate(channels)
    ]

    tri = (
        lax.broadcasted_iota(jnp.int32, (SPAN, SPAN), 0)
        >= lax.broadcasted_iota(jnp.int32, (SPAN, SPAN), 1)
    )
    ones = jnp.where(tri, 1.0, 0.0).astype(BF16)
    loads[0].wait()
    total = jnp.zeros((1, DK), F32)
    endings = []
    for b in range(blocks):
        r = dot(ones, g[b * SPAN : (b + 1) * SPAN, :])
        run[b] = r
        endings.append(r[SPAN - 1 : SPAN, :])
        ends[b : b + 1, :] = total
        total = total + endings[b]
    log_out[...] = total
    loads[1].wait()
    tail = jnp.zeros((1, DK), F32)
    for b in reversed(range(blocks)):
        part = slice(b * SPAN, (b + 1) * SPAN)
        kd[part, :] = (k[part, :].astype(F32) * jnp.exp((endings[b] - run[b]) + tail)).astype(BF16)
        tail = tail + endings[b]
    loads[2].wait()

    @pl.when(feeds)
    def _():
        pl.semaphore_wait(barrier, len(near))
        log_copy.start()

    for cols, core_copy in zip(channels, core_copies):
        grown = dot(kd[:, cols], v[...], ((0,), (0,)))
        own_state[cols, :] = grown
        core_out[cols, :] = grown.astype(BF16)
        pl.when(feeds)(core_copy.start)
    for load in loads[3:] + w_loads:
        load.start()

    @pl.when(feeds)
    def _():
        for copy in w_copies:
            copy.start()

    def lanes(row):
        return jnp.broadcast_to(row, (128, DK)).T

    def wide(columns):
        return jnp.concatenate([columns] * copies, axis=1)

    def part_of(z):
        return slice(z * part_rows, (z + 1) * part_rows)

    sum_copies = [
        remote(sum_out, sum_in.at[at_z], sum_send.at[0], sum_recv.at[0], device)
        for device in in_row
    ]
    tile_copies = [
        remote(tile_out.at[z], tile_in.at[at_z], tile_send.at[0], tile_recv.at[0], mate(at_x, z))
        for z in range(Z)
    ]
    row_copies = {
        dx: remote(row_out, row_in.at[at_x], row_send.at[0], row_recv.at[0], device)
        for dx, device in later.items()
    }
    total_copies = {
        dx: remote(total_out, total_in.at[at_x], total_send.at[0], total_recv.at[0], device)
        for dx, device in later.items()
    }
    enter_copies = [
        remote(enter_out.at[z], enter_in.at[at_z], enter_send.at[0], enter_recv.at[0], mate(at_x, z))
        for z in range(Z)
    ]
    pass_copy = remote(enter_in, carry, pass_send.at[0], pass_recv.at[0], sibling)

    @pl.when(scans)
    def _():
        log_copy.wait_recv()
        sum_out[...] = log_out[...] + log_in[...]
        decay[0] = lanes(jnp.exp(log_in[...]))
        decay[1] = lanes(jnp.exp(log_out[...]))
        sum_in[at_z] = sum_out[...]
        pl.semaphore_wait(barrier, len(near) + len(in_row) + len(later))
        for copy in sum_copies:
            copy.start()
        for i, core_copy in enumerate(core_copies):
            core_copy.wait_recv()
            for z in range(i * Z // 2, (i + 1) * Z // 2):
                part = part_of(z)
                tile_out[z] = (
                    wide(decay[1, part, :]) * core_in[part, :].astype(F32) + own_state[part, :]
                ).astype(BF16)
            for z in range(i * Z // 2, (i + 1) * Z // 2):
                pl.when(at_z != z)(tile_copies[z].start)
        tile_in[at_z] = tile_out[at_z]

    for load in loads[3:]:
        load.wait()
    state[...] = jnp.zeros_like(state)

    def local(b, _):
        part = pl.ds(pl.multiple_of(b * SPAN, SPAN), SPAN)
        r = run[b]
        middle = r[SPAN // 2 : SPAN // 2 + 1, :]
        ending = r[SPAN - 1 : SPAN, :]
        before = ends[pl.ds(b, 1), :]
        qf = q[part, :].astype(F32)
        kf = k[part, :].astype(F32)
        qi = qf * jnp.exp(r)
        qg[part, :] = (qi * jnp.exp(before)).astype(BF16)
        q_intra = (qf * jnp.exp(r - middle)).astype(BF16)
        k_intra = (kf * jnp.exp(middle - r)).astype(BF16)
        k_state = (kf * jnp.exp(ending - r)).astype(BF16)
        vb = v[part, :]
        scores = dot(q_intra, k_intra, ((1,), (1,)))
        weights = jnp.where(tri, scores, 0.0).astype(BF16)
        held = state[...]
        att[part, :] = dot(weights, vb) + dot(qi.astype(BF16), held.astype(BF16))
        state[...] = held * wide(lanes(jnp.exp(ending))) + dot(k_state, vb, ((0,), (0,)))
        of = o[part, :].astype(F32)
        act[part, :] = of / (1.0 + jnp.exp(-of)) * gain[...]
        return 0

    lax.fori_loop(0, blocks, local, 0)

    @pl.when(scans)
    def _():
        sums[...] = jnp.zeros_like(sums)
        landed(sum_in.at[0 : Z - 1], sum_recv.at[0])
        along = jnp.zeros((1, DK), F32)
        for z in range(Z):
            sums[z : z + 1, :] = sum_in[z]
            along = along + sum_in[z]
        row_out[...] = along
        for dx, copy in row_copies.items():
            pl.when(at_x + dx < rows_x)(copy.start)
        spans[...] = jnp.exp(sums[...].T)
        own_rows = pl.ds(pl.multiple_of(at_z * part_rows, part_rows), part_rows)

        def factor(table, i):
            return wide(jnp.broadcast_to(table[own_rows, :][:, i : i + 1], (part_rows, 128)))

        landed(tile_in.at[0 : Z - 1], tile_recv.at[0])
        grown = tile_in[0].astype(F32)
        for z in range(1, Z):
            grown = factor(spans, z) * grown + tile_in[z].astype(F32)
        total_out[...] = grown.astype(BF16)
        for dx, copy in total_copies.items():
            pl.when(at_x + dx < rows_x)(copy.start)
        ahead[...] = jnp.zeros_like(ahead)
        for x in range(1, rows_x):

            @pl.when(at_x == x)
            def _():
                landed(row_in.at[0:x], row_recv.at[0])
                for i in range(x):
                    sums[Z + i : Z + i + 1, :] = row_in[i]
                row_spans[...] = jnp.exp(sums[...].T)
                landed(total_in.at[0:x], total_recv.at[0])
                gone = total_in[0].astype(F32)
                for i in range(1, x):
                    gone = factor(row_spans, Z + i) * gone + total_in[i].astype(F32)
                ahead[...] = gone

        entry = ahead[...]
        for z in range(Z):
            enter_out[z] = entry.astype(BF16)
            if z < Z - 1:
                entry = factor(spans, z) * entry + tile_in[z].astype(F32)
        for z, copy in enumerate(enter_copies):
            pl.when(at_z != z)(copy.start)
        enter_in[at_z] = enter_out[at_z]
        landed(enter_in.at[0 : Z - 1], enter_recv.at[0])
        pass_copy.start()
        for z in range(Z):
            part = part_of(z)
            carry[z] = (
                wide(decay[0, part, :]) * enter_in[z].astype(F32) + core_in[part, :].astype(F32)
            ).astype(BF16)

    @pl.when(feeds)
    def _():
        for j, hand in zip((1, 0), hand_copies):
            landed(w_near.at[j], w_recv.at[j])
            hand.start()
        pass_copy.wait_recv()

    carried = carry[...].reshape(DK, DV)

    split = pieces // 2
    order = [i + j * split for i in range(split) for j in range(2)]
    parts = [slice(i * TOKENS, (i + 1) * TOKENS) for i in range(pieces)]
    g_copies = [
        remote(
            gated.at[0, parts[i], :], gated.at[1, parts[i], :], g_send.at[0], g_recv.at[i],
            near_a if i < split else near_b,
        )
        for i in range(pieces)
    ]
    y_copies = [
        remote(
            y_out.at[parts[i], :], y_in.at[parts[i], :], y_send.at[0], y_recv.at[i // 2],
            near_b if i < split else near_a,
        )
        for i in range(pieces)
    ]
    for i in order:
        part = parts[i]
        a = att[part, :] + dot(qg[part, :], carried)
        spread = jnp.mean(a * a, axis=-1, keepdims=True)
        gated[0, part, :] = (a * lax.rsqrt(spread + 1e-05) * act[part, :]).astype(BF16)
        g_copies[i].start()
    landed(w, w_sem.at[0])
    pl.when(scans)(lambda: landed(w_near, hand_recv.at[0]))

    for i in order:
        part = parts[i]
        g_copies[i].wait_recv()
        j = i // split
        y_out[part, :] = (
            dot(gated[0, part, :], w[2 - j]) + dot(gated[1, part, :], w_near[1, j])
        ).astype(BF16)
        y_copies[i].start()
    for i in order:
        part = parts[i]
        mine[part, :] = dot(gated[0, part, :], w[0]) + dot(gated[1, part, :], w_near[0, i // split])
    for i in (0, 2, 1, 3):
        part = slice(2 * i * TOKENS, 2 * (i + 1) * TOKENS)
        landed(y_in.at[part, :], y_recv.at[i])
        out[part, :] = (mine[part, :] + y_in[part, :].astype(F32)).astype(BF16)

    landed(gated.at[0], g_send.at[0])
    landed(y_out, y_send.at[0])

    @pl.when(feeds)
    def _():
        log_copy.wait_send()
        landed(core_out, core_send.at[0])
        landed(w_near, w_send.at[0])
        landed(w_near, hand_send.at[0])

    @pl.when(scans)
    def _():
        landed(sum_in.at[0 : Z - 1], sum_send.at[0])
        landed(tile_out.at[0 : Z - 1], tile_send.at[0])
        landed(enter_out.at[0 : Z - 1], enter_send.at[0])
        pass_copy.wait_send()
        for x in range(rows_x - 1):

            @pl.when(at_x == x)
            def _():
                landed(row_in.at[0 : rows_x - 1 - x], row_send.at[0])
                landed(total_in.at[0 : rows_x - 1 - x], total_send.at[0])


def shards(n_seq, n_head, queries, key_vectors, values, log_gate, out_gate, norm_gain, out_weight):
    length = queries.shape[0]
    width = out_weight.shape[1] // n_head
    blocks = length // SPAN
    pieces = length // TOKENS
    rows_x = n_seq // 2 // Z
    VM = pltpu.VMEM
    dma = pltpu.SemaphoreType.DMA
    tiles = VM((Z, DK // Z, DV), BF16)
    row = VM((1, DK), F32)
    scratch = [
        VM((length, DK), BF16), VM((length, DK), BF16), VM((length, DV), BF16),
        VM((length, DK), BF16), VM((length, DV), BF16), VM((1, DV), F32),
        VM((3, DV, width), BF16), VM((2, 2, DV, width), BF16),
        VM((blocks, SPAN, DK), F32), VM((blocks, DK), F32), VM((length, DK), BF16),
        VM((length, DK), BF16), VM((length, DV), F32), VM((length, DV), F32), VM((DK, DV), F32),
        row, row, VM((DK, DV), F32), VM((DK, DV), BF16), VM((DK, DV), BF16), VM((2, DK, 128), F32),
        row, VM((Z, 1, DK), F32), row, VM((rows_x, 1, DK), F32),
        VM((128, DK), F32), VM((DK, 128), F32), VM((DK, 128), F32),
        tiles, tiles, VM((DK // Z, DV), BF16), VM((rows_x, DK // Z, DV), BF16),
        VM((DK // Z, DV), F32), tiles, tiles, tiles,
        VM((2, length, DV), BF16), VM((length, width), F32),
        VM((length, width), BF16), VM((length, width), BF16),
        dma((6,)), dma((1,)), dma((1,)), dma((2,)), dma((1,)), dma((1,)),
        dma((1,)), dma((1,)), dma((1,)), dma((2,)),
        dma((1,)), dma((1,)), dma((1,)), dma((1,)), dma((1,)), dma((1,)),
        dma((1,)), dma((1,)), dma((1,)), dma((1,)), dma((1,)), dma((1,)),
        dma((1,)), dma((pieces,)), dma((1,)), dma((pieces // 2,)),
    ]
    return pl.pallas_call(
        functools.partial(kernel, n_seq, n_head),
        out_shape=pltpu.VMEM((length, width), BF16),
        in_specs=[pl.BlockSpec(memory_space=pl.ANY)] * 7,
        out_specs=pl.BlockSpec(memory_space=pltpu.VMEM),
        scratch_shapes=scratch,
        compiler_params=pltpu.CompilerParams(
            collective_id=0, has_side_effects=True, vmem_limit_bytes=56 * 2**20
        ),
        name="gated_layer",
    )(queries, key_vectors, values, log_gate, out_gate, norm_gain.reshape(1, DV), out_weight)


def solution(mesh):
    in_specs = (
        P("seq", "head"),
        P("seq", "head"),
        P("seq", "head"),
        P("seq", "head"),
        P("seq", "head"),
        P("head"),
        P("head", None),
    )
    out_specs = P("seq", "head")
    body = functools.partial(shards, mesh.shape["seq"], mesh.shape["head"])
    return jax.shard_map(body, mesh=mesh, in_specs=in_specs, out_specs=out_specs, check_vma=False)
```

time: 38.2 us -> 36.9 us (0.966)
  Pallas kernels: 37.3 us -> 35.7 us
    pallas_call x1, Pallas kernels: 37.3 us -> 35.7 us  [shards(): pl.pallas_call(functools.partial(kernel, n_seq, n_head), out_shape=pltpu....]
where the time goes in v3:
time: 36.9 us; the launch traced here: 36.5 us
  Pallas kernels  35.7 us (97%)
  local copies, waits for them, and re-layouts  0.8 us (2%)
    pallas_call x1, Pallas kernels, shards(): pl.pallas_call(functools.partial(kernel, n_seq, n_head), out_shape=pltpu....  35.7 us
    unnamed x1, local copies, waits for them, and re-layouts  0.8 us

profile of v3, /device:TPU:6, one launch (start us, length us, event | category | flops | bytes accessed | tf_op | source)
XLA Modules:
  0.0 36.5 jit_solution(17556173777327658116)
XLA Ops:
  0.0 35.7 %gated_layer.1 = bf16[512,512]{1,0:T(8,128)(2,1)S(1)} custom-call(bf16[512,256]{1,0:T(8,128)(2,1)} %q_hbm.1, bf16[512,256]{1,0:T(8,128)(2,1)} %k_hbm.1, bf16[512,512]{1,0:T(8,128)(2,1)} %v_hbm.1, bf16[512,256]{1,0:T(8,128)(2,1)} %g_hbm.1, bf16[512,512]{1,0:T(8,128)(2,1)} %o_hbm.1, f32[1,512]{1,0:T(1,128)} %bitcast.1, bf16[512,2048]{1,0:T(8,128)(2,1)} %w_hbm.1), custom_call_target="tpu_custom_call" | custom-call | tf_op jit(solution)/shard_map/gated_layer/pallas_call | solution.py:399
  35.7 0.8 %copy.9 = bf16[512,512]{1,0:T(8,128)(2,1)} copy(bf16[512,512]{1,0:T(8,128)(2,1)S(1)} %gated_layer.1) | data formatting | bytes 1048576

commit v4 on v3

--- a/solution.py
+++ b/solution.py
@@ -10,8 +10,9 @@
 DK = 256
 DV = 512
 SPAN = 64
-TOKENS = 64
+TOKENS = 128
 Z = 8
+EARLY = 3
 F32 = jnp.float32
 BF16 = jnp.bfloat16
 MESH = pl.DeviceIdType.MESH
@@ -169,9 +170,10 @@
         remote(sum_out, sum_in.at[at_z], sum_send.at[0], sum_recv.at[0], device)
         for device in in_row
     ]
+    far_first = [lax.rem(at_z + dz, Z) for dz in (4, 3, 5, 2, 6, 1, 7)]
     tile_copies = [
         remote(tile_out.at[z], tile_in.at[at_z], tile_send.at[0], tile_recv.at[0], mate(at_x, z))
-        for z in range(Z)
+        for z in far_first
     ]
     row_copies = {
         dx: remote(row_out, row_in.at[at_x], row_send.at[0], row_recv.at[0], device)
@@ -183,7 +185,7 @@
     }
     enter_copies = [
         remote(enter_out.at[z], enter_in.at[at_z], enter_send.at[0], enter_recv.at[0], mate(at_x, z))
-        for z in range(Z)
+        for z in list(range(EARLY)) + far_first
     ]
     pass_copy = remote(enter_in, carry, pass_send.at[0], pass_recv.at[0], sibling)
 
@@ -204,8 +206,8 @@
                 tile_out[z] = (
                     wide(decay[1, part, :]) * core_in[part, :].astype(F32) + own_state[part, :]
                 ).astype(BF16)
-            for z in range(i * Z // 2, (i + 1) * Z // 2):
-                pl.when(at_z != z)(tile_copies[z].start)
+        for copy in tile_copies:
+            copy.start()
         tile_in[at_z] = tile_out[at_z]
 
     for load in loads[3:]:
@@ -281,8 +283,10 @@
             enter_out[z] = entry.astype(BF16)
             if z < Z - 1:
                 entry = factor(spans, z) * entry + tile_in[z].astype(F32)
-        for z, copy in enumerate(enter_copies):
-            pl.when(at_z != z)(copy.start)
+        for z in range(EARLY):
+            pl.when(at_z != z)(enter_copies[z].start)
+        for z, copy in zip(far_first, enter_copies[EARLY:]):
+            pl.when(z >= EARLY)(copy.start)
         enter_in[at_z] = enter_out[at_z]
         landed(enter_in.at[0 : Z - 1], enter_recv.at[0])
         pass_copy.start()
@@ -338,7 +342,7 @@
     for i in order:
         part = parts[i]
         mine[part, :] = dot(gated[0, part, :], w[0]) + dot(gated[1, part, :], w_near[0, i // split])
-    for i in (0, 2, 1, 3):
+    for i in [i + j * split // 2 for i in range(split // 2) for j in range(2)]:
         part = slice(2 * i * TOKENS, 2 * (i + 1) * TOKENS)
         landed(y_in.at[part, :], y_recv.at[i])
         out[part, :] = (mine[part, :] + y_in[part, :].astype(F32)).astype(BF16)

time: 36.9 us -> 36.3 us (0.984)
  Pallas kernels: 35.7 us -> 35.3 us
    pallas_call x1, Pallas kernels: 35.7 us -> 35.3 us  [shards(): pl.pallas_call(functools.partial(kernel, n_seq, n_head), out_shape=pltpu....]
where the time goes in v4:
time: 36.3 us; the launch traced here: 36.1 us
  Pallas kernels  35.3 us (97%)
  local copies, waits for them, and re-layouts  0.8 us (2%)
    pallas_call x1, Pallas kernels, shards(): pl.pallas_call(functools.partial(kernel, n_seq, n_head), out_shape=pltpu....  35.3 us
    unnamed x1, local copies, waits for them, and re-layouts  0.8 us

profile of v4, /device:TPU:6, one launch (start us, length us, event | category | flops | bytes accessed | tf_op | source)
XLA Modules:
  0.0 36.1 jit_solution(11636176478001488670)
XLA Ops:
  0.0 35.3 %gated_layer.1 = bf16[512,512]{1,0:T(8,128)(2,1)S(1)} custom-call(bf16[512,256]{1,0:T(8,128)(2,1)} %q_hbm.1, bf16[512,256]{1,0:T(8,128)(2,1)} %k_hbm.1, bf16[512,512]{1,0:T(8,128)(2,1)} %v_hbm.1, bf16[512,256]{1,0:T(8,128)(2,1)} %g_hbm.1, bf16[512,512]{1,0:T(8,128)(2,1)} %o_hbm.1, f32[1,512]{1,0:T(1,128)} %bitcast.1, bf16[512,2048]{1,0:T(8,128)(2,1)} %w_hbm.1), custom_call_target="tpu_custom_call" | custom-call | tf_op jit(solution)/shard_map/gated_layer/pallas_call | solution.py:403
  35.3 0.8 %copy.9 = bf16[512,512]{1,0:T(8,128)(2,1)} copy(bf16[512,512]{1,0:T(8,128)(2,1)S(1)} %gated_layer.1) | data formatting | bytes 1048576

commit v5 on v4

--- a/solution.py
+++ b/solution.py
@@ -10,7 +10,7 @@
 DK = 256
 DV = 512
 SPAN = 64
-TOKENS = 128
+TOKENS = 64
 Z = 8
 EARLY = 3
 F32 = jnp.float32
@@ -30,7 +30,7 @@
     run, ends, kd, qg, att, act, state,
     log_out, log_in, own_state, core_out, core_in, decay,
     sum_out, sum_in, row_out, row_in, sums, spans, row_spans,
-    tile_out, tile_in, total_out, total_in, ahead, enter_out, enter_in, carry,
+    tile_out, tile_in, total_out, total_in, ahead, enter_out, enter_in, fac, lead,
     gated, mine, y_out, y_in,
     load_sem, w_sem, w_send, w_recv, hand_send, hand_recv,
     log_send, log_recv, core_send, core_recv,
@@ -187,14 +187,13 @@
         remote(enter_out.at[z], enter_in.at[at_z], enter_send.at[0], enter_recv.at[0], mate(at_x, z))
         for z in list(range(EARLY)) + far_first
     ]
-    pass_copy = remote(enter_in, carry, pass_send.at[0], pass_recv.at[0], sibling)
+    pass_copy = remote(enter_in, enter_in, pass_send.at[0], pass_recv.at[0], sibling)
 
     @pl.when(scans)
     def _():
         log_copy.wait_recv()
         sum_out[...] = log_out[...] + log_in[...]
-        decay[0] = lanes(jnp.exp(log_in[...]))
-        decay[1] = lanes(jnp.exp(log_out[...]))
+        decay[...] = lanes(jnp.exp(log_out[...]))
         sum_in[at_z] = sum_out[...]
         pl.semaphore_wait(barrier, len(near) + len(in_row) + len(later))
         for copy in sum_copies:
@@ -204,7 +203,7 @@
             for z in range(i * Z // 2, (i + 1) * Z // 2):
                 part = part_of(z)
                 tile_out[z] = (
-                    wide(decay[1, part, :]) * core_in[part, :].astype(F32) + own_state[part, :]
+                    wide(decay[part, :]) * core_in[part, :].astype(F32) + own_state[part, :]
                 ).astype(BF16)
         for copy in tile_copies:
             copy.start()
@@ -212,14 +211,24 @@
 
     for load in loads[3:]:
         load.wait()
-    state[...] = jnp.zeros_like(state)
+
+    @pl.when(feeds)
+    def _():
+        state[...] = jnp.zeros_like(state)
+        lead[...] = jnp.zeros_like(lead)
+
+    @pl.when(scans)
+    def _():
+        state[...] = core_in[...].astype(F32)
+        lead[...] = log_in[...]
+
 
     def local(b, _):
         part = pl.ds(pl.multiple_of(b * SPAN, SPAN), SPAN)
         r = run[b]
         middle = r[SPAN // 2 : SPAN // 2 + 1, :]
         ending = r[SPAN - 1 : SPAN, :]
-        before = ends[pl.ds(b, 1), :]
+        before = ends[pl.ds(b, 1), :] + lead[...]
         qf = q[part, :].astype(F32)
         kf = k[part, :].astype(F32)
         qi = qf * jnp.exp(r)
@@ -253,13 +262,15 @@
         spans[...] = jnp.exp(sums[...].T)
         own_rows = pl.ds(pl.multiple_of(at_z * part_rows, part_rows), part_rows)
 
-        def factor(table, i):
-            return wide(jnp.broadcast_to(table[own_rows, :][:, i : i + 1], (part_rows, 128)))
-
+        def spread(table, i):
+            fac[i] = jnp.broadcast_to(table[own_rows, :][:, i : i + 1], (part_rows, 128))
+
+        for z in range(Z):
+            spread(spans, z)
         landed(tile_in.at[0 : Z - 1], tile_recv.at[0])
         grown = tile_in[0].astype(F32)
         for z in range(1, Z):
-            grown = factor(spans, z) * grown + tile_in[z].astype(F32)
+            grown = wide(fac[z]) * grown + tile_in[z].astype(F32)
         total_out[...] = grown.astype(BF16)
         for dx, copy in total_copies.items():
             pl.when(at_x + dx < rows_x)(copy.start)
@@ -272,29 +283,26 @@
                 for i in range(x):
                     sums[Z + i : Z + i + 1, :] = row_in[i]
                 row_spans[...] = jnp.exp(sums[...].T)
+                for i in range(1, x):
+                    spread(row_spans, Z + i)
                 landed(total_in.at[0:x], total_recv.at[0])
                 gone = total_in[0].astype(F32)
                 for i in range(1, x):
-                    gone = factor(row_spans, Z + i) * gone + total_in[i].astype(F32)
+                    gone = wide(fac[Z + i]) * gone + total_in[i].astype(F32)
                 ahead[...] = gone
 
         entry = ahead[...]
         for z in range(Z):
             enter_out[z] = entry.astype(BF16)
+            if z < EARLY:
+                pl.when(at_z != z)(enter_copies[z].start)
             if z < Z - 1:
-                entry = factor(spans, z) * entry + tile_in[z].astype(F32)
-        for z in range(EARLY):
-            pl.when(at_z != z)(enter_copies[z].start)
+                entry = wide(fac[z]) * entry + tile_in[z].astype(F32)
         for z, copy in zip(far_first, enter_copies[EARLY:]):
             pl.when(z >= EARLY)(copy.start)
         enter_in[at_z] = enter_out[at_z]
         landed(enter_in.at[0 : Z - 1], enter_recv.at[0])
         pass_copy.start()
-        for z in range(Z):
-            part = part_of(z)
-            carry[z] = (
-                wide(decay[0, part, :]) * enter_in[z].astype(F32) + core_in[part, :].astype(F32)
-            ).astype(BF16)
 
     @pl.when(feeds)
     def _():
@@ -303,7 +311,7 @@
             hand.start()
         pass_copy.wait_recv()
 
-    carried = carry[...].reshape(DK, DV)
+    carried = enter_in[...].reshape(DK, DV)
 
     split = pieces // 2
     order = [i + j * split for i in range(split) for j in range(2)]
@@ -387,11 +395,11 @@
         VM((3, DV, width), BF16), VM((2, 2, DV, width), BF16),
         VM((blocks, SPAN, DK), F32), VM((blocks, DK), F32), VM((length, DK), BF16),
         VM((length, DK), BF16), VM((length, DV), F32), VM((length, DV), F32), VM((DK, DV), F32),
-        row, row, VM((DK, DV), F32), VM((DK, DV), BF16), VM((DK, DV), BF16), VM((2, DK, 128), F32),
+        row, row, VM((DK, DV), F32), VM((DK, DV), BF16), VM((DK, DV), BF16), VM((DK, 128), F32),
         row, VM((Z, 1, DK), F32), row, VM((rows_x, 1, DK), F32),
         VM((128, DK), F32), VM((DK, 128), F32), VM((DK, 128), F32),
         tiles, tiles, VM((DK // Z, DV), BF16), VM((rows_x, DK // Z, DV), BF16),
-        VM((DK // Z, DV), F32), tiles, tiles, tiles,
+        VM((DK // Z, DV), F32), tiles, tiles, VM((Z + rows_x, DK // Z, 128), F32), row,
         VM((2, length, DV), BF16), VM((length, width), F32),
         VM((length, width), BF16), VM((length, width), BF16),
         dma((6,)), dma((1,)), dma((1,)), dma((2,)), dma((1,)), dma((1,)),

time: 36.3 us -> 36 us (level)
  no operation moved by 1% of the time
where the time goes in v5:
time: 36 us; the launch traced here: 35.8 us
  Pallas kernels  35 us (97%)
  local copies, waits for them, and re-layouts  0.8 us (2%)
    pallas_call x1, Pallas kernels, shards(): pl.pallas_call(functools.partial(kernel, n_seq, n_head), out_shape=pltpu....  35 us
    unnamed x1, local copies, waits for them, and re-layouts  0.8 us

profile of v5, /device:TPU:6, one launch (start us, length us, event | category | flops | bytes accessed | tf_op | source)
XLA Modules:
  0.0 35.8 jit_solution(14427369436068651591)
XLA Ops:
  0.0 35.0 %gated_layer.1 = bf16[512,512]{1,0:T(8,128)(2,1)S(1)} custom-call(bf16[512,256]{1,0:T(8,128)(2,1)} %q_hbm.1, bf16[512,256]{1,0:T(8,128)(2,1)} %k_hbm.1, bf16[512,512]{1,0:T(8,128)(2,1)} %v_hbm.1, bf16[512,256]{1,0:T(8,128)(2,1)} %g_hbm.1, bf16[512,512]{1,0:T(8,128)(2,1)} %o_hbm.1, f32[1,512]{1,0:T(1,128)} %bitcast.1, bf16[512,2048]{1,0:T(8,128)(2,1)} %w_hbm.1), custom_call_target="tpu_custom_call" | custom-call | tf_op jit(solution)/shard_map/gated_layer/pallas_call | solution.py:411
  35.0 0.8 %copy.9 = bf16[512,512]{1,0:T(8,128)(2,1)} copy(bf16[512,512]{1,0:T(8,128)(2,1)S(1)} %gated_layer.1) | data formatting | bytes 1048576

commit v6 on v5

--- a/solution.py
+++ b/solution.py
@@ -32,11 +32,10 @@
     sum_out, sum_in, row_out, row_in, sums, spans, row_spans,
     tile_out, tile_in, total_out, total_in, ahead, enter_out, enter_in, fac, lead,
     gated, mine, y_out, y_in,
-    load_sem, w_sem, w_send, w_recv, hand_send, hand_recv,
-    log_send, log_recv, core_send, core_recv,
+    load_sem, w_sem, hand_sem, log_sem, core_sem, pass_sem,
     sum_send, sum_recv, row_send, row_recv, tile_send, tile_recv,
-    total_send, total_recv, enter_send, enter_recv, pass_send, pass_recv,
-    g_send, g_recv, y_send, y_recv,
+    total_send, total_recv, enter_send, enter_recv,
+    g_recv, y_send, y_recv,
 ):
     loads = [
         pltpu.make_async_copy(src, dst, load_sem.at[i])
@@ -100,21 +99,17 @@
         for j, which in enumerate((head, head_a, head_b))
     ]
     w_copies = [
-        remote(w_hbm.at[:, columns(which)], w_near.at[j, i], w_send.at[0], w_recv.at[j], device)
+        remote(w_hbm.at[:, columns(which)], w_near.at[j, i], sum_send.at[0], (sum_recv, tile_recv)[j].at[0], device)
         for which, j, i, device in (
             (head_c, 1, 0, near_a), (head_c, 1, 1, near_b),
             (head_a, 0, 0, near_a), (head_b, 0, 1, near_b),
         )
     ]
     hand_copies = [
-        remote(w_near.at[j], w_near.at[j], hand_send.at[0], hand_recv.at[0], sibling) for j in (1, 0)
-    ]
-    log_copy = remote(log_out, log_in, log_send.at[0], log_recv.at[0], sibling)
-    channels = [slice(0, DK // 2), slice(DK // 2, DK)]
-    core_copies = [
-        remote(core_out.at[cols, :], core_in.at[cols, :], core_send.at[0], core_recv.at[i], sibling)
-        for i, cols in enumerate(channels)
-    ]
+        remote(w_near.at[j], w_near.at[j], hand_sem.at[0], hand_sem.at[0], sibling) for j in (1, 0)
+    ]
+    log_copy = remote(log_out, log_in, log_sem.at[0], log_sem.at[0], sibling)
+    core_copy = remote(core_out, core_in, core_sem.at[0], core_sem.at[0], sibling)
 
     tri = (
         lax.broadcasted_iota(jnp.int32, (SPAN, SPAN), 0)
@@ -144,11 +139,10 @@
         pl.semaphore_wait(barrier, len(near))
         log_copy.start()
 
-    for cols, core_copy in zip(channels, core_copies):
-        grown = dot(kd[:, cols], v[...], ((0,), (0,)))
-        own_state[cols, :] = grown
-        core_out[cols, :] = grown.astype(BF16)
-        pl.when(feeds)(core_copy.start)
+    grown = dot(kd[...], v[...], ((0,), (0,)))
+    own_state[...] = grown
+    core_out[...] = grown.astype(BF16)
+    pl.when(feeds)(core_copy.start)
     for load in loads[3:] + w_loads:
         load.start()
 
@@ -187,7 +181,7 @@
         remote(enter_out.at[z], enter_in.at[at_z], enter_send.at[0], enter_recv.at[0], mate(at_x, z))
         for z in list(range(EARLY)) + far_first
     ]
-    pass_copy = remote(enter_in, enter_in, pass_send.at[0], pass_recv.at[0], sibling)
+    pass_copy = remote(enter_in, enter_in, pass_sem.at[0], pass_sem.at[0], sibling)
 
     @pl.when(scans)
     def _():
@@ -198,13 +192,12 @@
         pl.semaphore_wait(barrier, len(near) + len(in_row) + len(later))
         for copy in sum_copies:
             copy.start()
-        for i, core_copy in enumerate(core_copies):
-            core_copy.wait_recv()
-            for z in range(i * Z // 2, (i + 1) * Z // 2):
-                part = part_of(z)
-                tile_out[z] = (
-                    wide(decay[part, :]) * core_in[part, :].astype(F32) + own_state[part, :]
-                ).astype(BF16)
+        core_copy.wait_recv()
+        for z in range(Z):
+            part = part_of(z)
+            tile_out[z] = (
+                wide(decay[part, :]) * core_in[part, :].astype(F32) + own_state[part, :]
+            ).astype(BF16)
         for copy in tile_copies:
             copy.start()
         tile_in[at_z] = tile_out[at_z]
@@ -307,7 +300,7 @@
     @pl.when(feeds)
     def _():
         for j, hand in zip((1, 0), hand_copies):
-            landed(w_near.at[j], w_recv.at[j])
+            landed(w_near.at[j], (sum_recv, tile_recv)[j].at[0])
             hand.start()
         pass_copy.wait_recv()
 
@@ -318,14 +311,14 @@
     parts = [slice(i * TOKENS, (i + 1) * TOKENS) for i in range(pieces)]
     g_copies = [
         remote(
-            gated.at[0, parts[i], :], gated.at[1, parts[i], :], g_send.at[0], g_recv.at[i],
+            gated.at[0, parts[i], :], gated.at[1, parts[i], :], y_send.at[0], g_recv.at[i],
             near_a if i < split else near_b,
         )
         for i in range(pieces)
     ]
     y_copies = [
         remote(
-            y_out.at[parts[i], :], y_in.at[parts[i], :], y_send.at[0], y_recv.at[i // 2],
+            y_out.at[parts[i], :], y_in.at[parts[i], :], y_send.at[0], y_recv.at[i // 4],
             near_b if i < split else near_a,
         )
         for i in range(pieces)
@@ -337,7 +330,7 @@
         gated[0, part, :] = (a * lax.rsqrt(spread + 1e-05) * act[part, :]).astype(BF16)
         g_copies[i].start()
     landed(w, w_sem.at[0])
-    pl.when(scans)(lambda: landed(w_near, hand_recv.at[0]))
+    pl.when(scans)(lambda: landed(w_near, hand_sem.at[0]))
 
     for i in order:
         part = parts[i]
@@ -350,20 +343,19 @@
     for i in order:
         part = parts[i]
         mine[part, :] = dot(gated[0, part, :], w[0]) + dot(gated[1, part, :], w_near[0, i // split])
-    for i in [i + j * split // 2 for i in range(split // 2) for j in range(2)]:
-        part = slice(2 * i * TOKENS, 2 * (i + 1) * TOKENS)
+    for i in range(2):
+        part = slice(i * split * TOKENS, (i + 1) * split * TOKENS)
         landed(y_in.at[part, :], y_recv.at[i])
         out[part, :] = (mine[part, :] + y_in[part, :].astype(F32)).astype(BF16)
 
-    landed(gated.at[0], g_send.at[0])
-    landed(y_out, y_send.at[0])
+    landed(gated, y_send.at[0])
 
     @pl.when(feeds)
     def _():
         log_copy.wait_send()
-        landed(core_out, core_send.at[0])
-        landed(w_near, w_send.at[0])
-        landed(w_near, hand_send.at[0])
+        core_copy.wait_send()
+        landed(w_near, sum_send.at[0])
+        landed(w_near, hand_sem.at[0])
 
     @pl.when(scans)
     def _():
@@ -402,11 +394,10 @@
         VM((DK // Z, DV), F32), tiles, tiles, VM((Z + rows_x, DK // Z, 128), F32), row,
         VM((2, length, DV), BF16), VM((length, width), F32),
         VM((length, width), BF16), VM((length, width), BF16),
-        dma((6,)), dma((1,)), dma((1,)), dma((2,)), dma((1,)), dma((1,)),
-        dma((1,)), dma((1,)), dma((1,)), dma((2,)),
+        dma((6,)), dma((1,)), dma((1,)), dma((1,)), dma((1,)), dma((1,)),
         dma((1,)), dma((1,)), dma((1,)), dma((1,)), dma((1,)), dma((1,)),
-        dma((1,)), dma((1,)), dma((1,)), dma((1,)), dma((1,)), dma((1,)),
-        dma((1,)), dma((pieces,)), dma((1,)), dma((pieces // 2,)),
+        dma((1,)), dma((1,)), dma((1,)), dma((1,)),
+        dma((pieces,)), dma((1,)), dma((pieces // 4,)),
     ]
     return pl.pallas_call(
         functools.partial(kernel, n_seq, n_head),

time: 36 us -> 36 us (level)
  no operation moved by 1% of the time
where the time goes in v6:
time: 36 us; the launch traced here: 35.7 us
  Pallas kernels  34.9 us (97%)
  local copies, waits for them, and re-layouts  0.8 us (2%)
    pallas_call x1, Pallas kernels, shards(): pl.pallas_call(functools.partial(kernel, n_seq, n_head), out_shape=pltpu....  34.9 us
    unnamed x1, local copies, waits for them, and re-layouts  0.8 us

profile of v6, /device:TPU:6, one launch (start us, length us, event | category | flops | bytes accessed | tf_op | source)
XLA Modules:
  0.0 35.7 jit_solution(15594956062022430616)
XLA Ops:
  0.0 34.9 %gated_layer.1 = bf16[512,512]{1,0:T(8,128)(2,1)S(1)} custom-call(bf16[512,256]{1,0:T(8,128)(2,1)} %q_hbm.1, bf16[512,256]{1,0:T(8,128)(2,1)} %k_hbm.1, bf16[512,512]{1,0:T(8,128)(2,1)} %v_hbm.1, bf16[512,256]{1,0:T(8,128)(2,1)} %g_hbm.1, bf16[512,512]{1,0:T(8,128)(2,1)} %o_hbm.1, f32[1,512]{1,0:T(1,128)} %bitcast.1, bf16[512,2048]{1,0:T(8,128)(2,1)} %w_hbm.1), custom_call_target="tpu_custom_call" | custom-call | tf_op jit(solution)/shard_map/gated_layer/pallas_call | solution.py:402
  34.9 0.8 %copy.9 = bf16[512,512]{1,0:T(8,128)(2,1)} copy(bf16[512,512]{1,0:T(8,128)(2,1)S(1)} %gated_layer.1) | data formatting | bytes 1048576

commit v7 on v6

--- a/solution.py
+++ b/solution.py
@@ -70,7 +70,7 @@
     def mate(x, z):
         return {"seq": (x * Z + z) * 2 + core, "head": head}
 
-    in_row = [mate(at_x, lax.rem(at_z + dz, Z)) for dz in range(1, Z)]
+    in_row = [mate(at_x, lax.rem(at_z + dz, Z)) for dz in (4, 3, 5, 2, 6, 1, 7)]
     later = {dx: mate(lax.rem(at_x + dx, rows_x), at_z) for dx in (2, 1, 3)}
 
     def columns(which):
@@ -140,9 +140,16 @@
         log_copy.start()
 
     grown = dot(kd[...], v[...], ((0,), (0,)))
-    own_state[...] = grown
-    core_out[...] = grown.astype(BF16)
-    pl.when(feeds)(core_copy.start)
+
+    @pl.when(feeds)
+    def _():
+        core_out[...] = grown.astype(BF16)
+        core_copy.start()
+
+    @pl.when(scans)
+    def _():
+        own_state[...] = grown
+
     for load in loads[3:] + w_loads:
         load.start()
 
@@ -187,11 +194,11 @@
     def _():
         log_copy.wait_recv()
         sum_out[...] = log_out[...] + log_in[...]
-        decay[...] = lanes(jnp.exp(log_out[...]))
-        sum_in[at_z] = sum_out[...]
         pl.semaphore_wait(barrier, len(near) + len(in_row) + len(later))
         for copy in sum_copies:
             copy.start()
+        decay[...] = lanes(jnp.exp(log_out[...]))
+        sum_in[at_z] = sum_out[...]
         core_copy.wait_recv()
         for z in range(Z):
             part = part_of(z)

time: 36 us -> 36 us (level)
  no operation moved by 1% of the time
where the time goes in v7:
time: 36 us; the launch traced here: 35.7 us
  Pallas kernels  34.9 us (97%)
  local copies, waits for them, and re-layouts  0.8 us (2%)
    pallas_call x1, Pallas kernels, shards(): pl.pallas_call(functools.partial(kernel, n_seq, n_head), out_shape=pltpu....  34.9 us
    unnamed x1, local copies, waits for them, and re-layouts  0.8 us

profile of v7, /device:TPU:6, one launch (start us, length us, event | category | flops | bytes accessed | tf_op | source)
XLA Modules:
  0.0 35.7 jit_solution(17534195887249426788)
XLA Ops:
  0.0 34.9 %gated_layer.1 = bf16[512,512]{1,0:T(8,128)(2,1)S(1)} custom-call(bf16[512,256]{1,0:T(8,128)(2,1)} %q_hbm.1, bf16[512,256]{1,0:T(8,128)(2,1)} %k_hbm.1, bf16[512,512]{1,0:T(8,128)(2,1)} %v_hbm.1, bf16[512,256]{1,0:T(8,128)(2,1)} %g_hbm.1, bf16[512,512]{1,0:T(8,128)(2,1)} %o_hbm.1, f32[1,512]{1,0:T(1,128)} %bitcast.1, bf16[512,2048]{1,0:T(8,128)(2,1)} %w_hbm.1), custom_call_target="tpu_custom_call" | custom-call | tf_op jit(solution)/shard_map/gated_layer/pallas_call | solution.py:409
  35.0 0.8 %copy.9 = bf16[512,512]{1,0:T(8,128)(2,1)} copy(bf16[512,512]{1,0:T(8,128)(2,1)S(1)} %gated_layer.1) | data formatting | bytes 1048576

commit v8 on v7

--- a/solution.py
+++ b/solution.py
@@ -10,7 +10,7 @@
 DK = 256
 DV = 512
 SPAN = 64
-TOKENS = 64
+TOKENS = 128
 Z = 8
 EARLY = 3
 F32 = jnp.float32
@@ -325,7 +325,7 @@
     ]
     y_copies = [
         remote(
-            y_out.at[parts[i], :], y_in.at[parts[i], :], y_send.at[0], y_recv.at[i // 4],
+            y_out.at[parts[i], :], y_in.at[parts[i], :], y_send.at[0], y_recv.at[i // split],
             near_b if i < split else near_a,
         )
         for i in range(pieces)
@@ -404,7 +404,7 @@
         dma((6,)), dma((1,)), dma((1,)), dma((1,)), dma((1,)), dma((1,)),
         dma((1,)), dma((1,)), dma((1,)), dma((1,)), dma((1,)), dma((1,)),
         dma((1,)), dma((1,)), dma((1,)), dma((1,)),
-        dma((pieces,)), dma((1,)), dma((pieces // 4,)),
+        dma((pieces,)), dma((1,)), dma((2,)),
     ]
     return pl.pallas_call(
         functools.partial(kernel, n_seq, n_head),

time: 36 us -> 36 us (level)
  no operation moved by 1% of the time
where the time goes in v8:
time: 36 us; the launch traced here: 35.7 us
  Pallas kernels  34.9 us (97%)
  local copies, waits for them, and re-layouts  0.8 us (2%)
    pallas_call x1, Pallas kernels, shards(): pl.pallas_call(functools.partial(kernel, n_seq, n_head), out_shape=pltpu....  34.9 us
    unnamed x1, local copies, waits for them, and re-layouts  0.8 us

profile of v8, /device:TPU:6, one launch (start us, length us, event | category | flops | bytes accessed | tf_op | source)
XLA Modules:
  0.0 35.7 jit_solution(243865851246778174)
XLA Ops:
  0.0 34.9 %gated_layer.1 = bf16[512,512]{1,0:T(8,128)(2,1)S(1)} custom-call(bf16[512,256]{1,0:T(8,128)(2,1)} %q_hbm.1, bf16[512,256]{1,0:T(8,128)(2,1)} %k_hbm.1, bf16[512,512]{1,0:T(8,128)(2,1)} %v_hbm.1, bf16[512,256]{1,0:T(8,128)(2,1)} %g_hbm.1, bf16[512,512]{1,0:T(8,128)(2,1)} %o_hbm.1, f32[1,512]{1,0:T(1,128)} %bitcast.1, bf16[512,2048]{1,0:T(8,128)(2,1)} %w_hbm.1), custom_call_target="tpu_custom_call" | custom-call | tf_op jit(solution)/shard_map/gated_layer/pallas_call | solution.py:409
  35.0 0.8 %copy.9 = bf16[512,512]{1,0:T(8,128)(2,1)} copy(bf16[512,512]{1,0:T(8,128)(2,1)S(1)} %gated_layer.1) | data formatting | bytes 1048576

commit v9 on v7

--- a/solution.py
+++ b/solution.py
@@ -126,6 +126,12 @@
         ends[b : b + 1, :] = total
         total = total + endings[b]
     log_out[...] = total
+
+    @pl.when(feeds)
+    def _():
+        pl.semaphore_wait(barrier, len(near))
+        log_copy.start()
+
     loads[1].wait()
     tail = jnp.zeros((1, DK), F32)
     for b in reversed(range(blocks)):
@@ -133,11 +139,6 @@
         kd[part, :] = (k[part, :].astype(F32) * jnp.exp((endings[b] - run[b]) + tail)).astype(BF16)
         tail = tail + endings[b]
     loads[2].wait()
-
-    @pl.when(feeds)
-    def _():
-        pl.semaphore_wait(barrier, len(near))
-        log_copy.start()
 
     grown = dot(kd[...], v[...], ((0,), (0,)))
 

time: 36 us -> 35.9 us (level)
  no operation moved by 1% of the time
where the time goes in v9:
time: 35.9 us; the launch traced here: 35.7 us
  Pallas kernels  34.9 us (97%)
  local copies, waits for them, and re-layouts  0.8 us (2%)
    pallas_call x1, Pallas kernels, shards(): pl.pallas_call(functools.partial(kernel, n_seq, n_head), out_shape=pltpu....  34.9 us
    unnamed x1, local copies, waits for them, and re-layouts  0.8 us

profile of v9, /device:TPU:6, one launch (start us, length us, event | category | flops | bytes accessed | tf_op | source)
XLA Modules:
  0.0 35.7 jit_solution(16302419002055797275)
XLA Ops:
  0.0 34.9 %gated_layer.1 = bf16[512,512]{1,0:T(8,128)(2,1)S(1)} custom-call(bf16[512,256]{1,0:T(8,128)(2,1)} %q_hbm.1, bf16[512,256]{1,0:T(8,128)(2,1)} %k_hbm.1, bf16[512,512]{1,0:T(8,128)(2,1)} %v_hbm.1, bf16[512,256]{1,0:T(8,128)(2,1)} %g_hbm.1, bf16[512,512]{1,0:T(8,128)(2,1)} %o_hbm.1, f32[1,512]{1,0:T(1,128)} %bitcast.1, bf16[512,2048]{1,0:T(8,128)(2,1)} %w_hbm.1), custom_call_target="tpu_custom_call" | custom-call | tf_op jit(solution)/shard_map/gated_layer/pallas_call | solution.py:410
  34.9 0.8 %copy.9 = bf16[512,512]{1,0:T(8,128)(2,1)} copy(bf16[512,512]{1,0:T(8,128)(2,1)S(1)} %gated_layer.1) | data formatting | bytes 1048576
